TPU v7x, 128 devices: a whole 4x4x4 slice. The times are simulated.
128 devices in a mesh: rows: 32 (over y, z, core), tgt: 4 (over x).
Axes of the slice: x: 4, y: 4, z: 4, core: 2. Of those that a mesh axis runs over, the one named last changes fastest.
Arguments:
- frames: bfloat16 [65536, 512], P('rows', 'tgt'), may hold values from -6 to 6
- weights: bfloat16 [512, 1024], replicated, may hold values from -0.25 to 0.25
- phases: float32 [1024], replicated, may hold values from -3.140625 to 3.140625
- residual: float32 [65536, 1024], P('rows', 'tgt'), may hold values from -6 to 6
Outputs:
- residual_next: float32 [65536, 1024], P('rows', 'tgt')
- coefficients: float32 [1024, 1024], P(None, 'tgt')
All inputs are finite; a program needn't handle non-finite values.
Results may differ from a plain program's by a relative error of at most 0.0003.
Values may be sent and summed in bfloat16 or wider, within the bound.
No kernel may reach another device: no remote copies, remote signals or barrier semaphores. Data moves between devices by JAX's collectives and lax.ppermute only.
A program may use at most 128 MiB of HBM per device.

v0:
```python
import math

import jax
import jax.numpy as jnp
from jax import lax
from jax.experimental import pallas as pl
from jax.experimental.pallas import tpu as pltpu
from jax.sharding import PartitionSpec as P


F32 = jnp.float32
BF16 = jnp.bfloat16
HIGHEST = lax.Precision.HIGHEST
NB = 128
PB = 16
SIN_PI = (
    3.1415926535362892,
    -5.167712764624528,
    2.5501633189472983,
    -0.5992521978285216,
    0.08205040183240117,
    -0.007028386446239114,
)


def dot(a, b, precision=None):
    return lax.dot_general(
        a, b, (((1,), (0,)), ((), ())), precision=precision, preferred_element_type=F32
    )


def dot_t(a, b, precision=None):
    return lax.dot_general(
        a, b, (((0,), (0,)), ((), ())), precision=precision, preferred_element_type=F32
    )


def split2(x):
    high = x.astype(BF16)
    return high, (x - high.astype(F32)).astype(BF16)


def split3(x):
    high = x.astype(BF16)
    rest = x - high.astype(F32)
    mid = rest.astype(BF16)
    return high, mid, (rest - mid.astype(F32)).astype(BF16)


def dot3(a, b):
    return dot(a[0], b[0]) + (dot(a[0], b[1]) + dot(a[1], b[0]))


def dot3_t(a, b):
    return dot_t(a[0], b[0]) + (dot_t(a[0], b[1]) + dot_t(a[1], b[0]))


def features(frames, weights, phases):
    turns = (dot(frames, weights) + phases) * (0.5 / math.pi)
    r = turns - jnp.round(turns)
    s = r * r
    poly = jnp.full_like(s, SIN_PI[-1])
    for coef in SIN_PI[-2::-1]:
        poly = poly * s + coef
    half = poly * r
    scale = math.sqrt(2.0 / weights.shape[1])
    return scale - (2.0 * scale) * (half * half)


def packed_slot(block, blocks):
    if block < blocks // 2:
        return block, 0
    return blocks - 1 - block, (block + 1) * NB


def gram_kernel(frames, weights, phases, out, high, low):
    blocks = out.shape[0] * 2
    slabs = jnp.concatenate([frames[i] for i in range(frames.shape[0])], axis=1)
    h, l = split2(features(slabs, weights[...], phases[...]))
    high[...] = h
    low[...] = l
    for i in range(blocks):
        rows = slice(i * NB, (i + 1) * NB)
        right = slice(i * NB, blocks * NB)
        g = dot_t(high[:, rows], high[:, right])
        g = g + dot_t(high[:, rows], low[:, right])
        g = g + dot_t(low[:, rows], high[:, right])
        at, col = packed_slot(i, blocks)
        out[at, :, col : col + (blocks - i) * NB] = g


def feature_kernel(order, *refs):
    tops, bottoms, (weights, phases, residual, high, low, corr) = refs[:4], refs[4:8], refs[8:]
    below = pl.program_id(0) >= pl.num_programs(0) // 2
    slabs = [jnp.where(below, b[...], t[...]) for t, b in zip(tops, bottoms)]
    sorted_weights = jnp.concatenate([weights[order[i]] for i in range(4)], axis=0)
    h, l = split2(features(jnp.concatenate(slabs, axis=1), sorted_weights, phases[...]))
    high[...] = h
    low[...] = l
    right = split2(residual[...])
    part = dot3_t((h, l), right)

    @pl.when(pl.program_id(0) == 0)
    def _():
        corr[...] = part

    @pl.when(pl.program_id(0) > 0)
    def _():
        corr[...] += part


def invert_block(d):
    lane = lax.broadcasted_iota(jnp.int32, (PB, NB), 1)
    sub = lax.broadcasted_iota(jnp.int32, (PB, NB), 0)
    col_at = lax.broadcasted_iota(jnp.int32, (NB, NB), 1)
    zero = jnp.zeros((PB, NB), F32)
    for k0 in range(0, NB, PB):
        rows = d[k0 : k0 + PB, :]
        cols = [jnp.broadcast_to(rows[:, k0 + j : k0 + j + 1], (PB, NB)) for j in range(PB)]
        lh, lm, ll = split3(jnp.where(lane < k0, -rows, rows))
        left = jnp.concatenate([lh, lh, lm, lm, lh, ll], axis=0)
        x = jnp.where((lane >= k0) & (lane < k0 + PB), jnp.where(lane - k0 == sub, 1.0, 0.0), rows)
        scale = zero
        for k in range(PB):
            c = cols[k]
            p = 1.0 / c[k : k + 1, :]
            m = jnp.where(sub == k, 0.0, c * p)
            scale = jnp.where(sub == k, p, scale)
            for j in range(k + 1, PB):
                cols[j] = cols[j] - m * cols[j][k : k + 1, :]
            x = x - m * x[k : k + 1, :]
        x = x * scale
        xh, xm, xl = split3(x)
        right = jnp.concatenate([xh, xm, xh, xm, xl, xh], axis=0)
        update = dot_t(left, right)
        kept = d[...]
        d[...] = jnp.where((col_at >= k0) & (col_at < k0 + PB), 0.0, kept) - update
        d[k0 : k0 + PB, :] = x


def factor_steps(rows_of, panel, inverse, left, d, ridge):
    steps, _, width = panel[0].shape
    for ref in (*panel, *left):
        ref[...] = jnp.zeros_like(ref)
    eye = jnp.where(
        lax.broadcasted_iota(jnp.int32, (NB, NB), 0) == lax.broadcasted_iota(jnp.int32, (NB, NB), 1),
        ridge,
        0.0,
    ).astype(F32)

    def step(i, _):
        own = pl.ds(pl.multiple_of(i * NB, NB), NB)
        before = [ref[:, :, own].reshape(steps * NB, NB) for ref in left]
        done = [ref[...].reshape(steps * NB, width) for ref in panel]
        here = [ref[:, :, own].reshape(steps * NB, NB) for ref in panel]
        d[...] = rows_of(i, own) - dot3_t(before, here) + eye
        row = rows_of(i, slice(None)) - dot3_t(before, done)
        parts = split2(row)
        invert_block(d)
        inverse[i] = d[...]
        result = split2(dot(d[...], row, HIGHEST))
        for k in range(2):
            left[k][i] = parts[k]
            panel[k][i] = result[k]
        return 0

    lax.fori_loop(0, steps, step, 0)


def first_factor_kernel(core, mine, other, high, low, inverse, rest, a, lh, ll, d, *, ridge):
    blocks = a.shape[0]
    size = blocks * NB
    quarter = blocks // 4
    steps = high.shape[0]

    def unpack(halves):
        for i in range(blocks):
            at, col = packed_slot(i, blocks)
            a[i, :, i * NB : size] = halves[at // quarter][at % quarter, :, col : col + size - i * NB]

    @pl.when(core[0] == 0)
    def _():
        unpack((mine, other))

    @pl.when(core[0] != 0)
    def _():
        unpack((other, mine))

    for i in range(1, blocks):
        a[i, :, : i * NB] = jnp.zeros((NB, i * NB), F32)
    factor_steps(lambda i, cols: a[i, :, cols], (high, low), inverse, (lh, ll), d, ridge)
    edge = steps * NB
    right = [ref[:, :, edge:].reshape(edge, size - edge) for ref in (high, low)]
    for i in range(steps, blocks):
        cols = slice(i * NB, (i + 1) * NB)
        before = [ref[:, :, cols].reshape(edge, NB) for ref in (lh, ll)]
        rest[i - steps] = a[i, :, edge:] - dot3_t(before, right)


def second_factor_kernel(matrix, high, low, inverse, lh, ll, d, *, ridge):
    factor_steps(lambda i, cols: matrix[i, :, cols], (high, low), inverse, (lh, ll), d, ridge)


def solve_kernel(high0, low0, inverse0, high1, low1, inverse1, corr, out, ch, cl, wh, wl):
    half = high0.shape[0]
    blocks = half + high1.shape[0]
    edge = half * NB

    def store(parts, rows, value):
        for ref, part in zip(parts, split2(value)):
            ref[rows, :] = part

    def known(parts, first, last):
        return [ref[first * NB : last * NB, :] for ref in parts]

    for i in range(blocks):
        rows = slice(i * NB, (i + 1) * NB)
        value = corr[rows, :]
        top = min(i, half)
        if top > 0:
            left = [ref[:top, :, rows].reshape(top * NB, NB) for ref in (high0, low0)]
            value = value - dot3_t(left, known((ch, cl), 0, top))
        if i > half:
            cols = slice(i * NB - edge, (i + 1) * NB - edge)
            left = [ref[: i - half, :, cols].reshape((i - half) * NB, NB) for ref in (high1, low1)]
            value = value - dot3_t(left, known((ch, cl), half, i))
        store((ch, cl), rows, value)
    for i in range(blocks - 1, -1, -1):
        rows = slice(i * NB, (i + 1) * NB)
        inverse = inverse0[i] if i < half else inverse1[i - half]
        value = dot3(split2(inverse), known((ch, cl), i, i + 1))
        if i < blocks - 1:
            panel = (high0, low0) if i < half else (high1, low1)
            base = 0 if i < half else half
            right = [ref[i - base, :, (i + 1 - base) * NB :] for ref in panel]
            value = value - dot3(right, known((wh, wl), i + 1, blocks))
        out[rows, :] = value
        store((wh, wl), rows, value)


def update_kernel(high, low, coef, residual, out):
    wh, wl = split2(coef[...])
    h = high[...]
    out[...] = residual[...] - (dot(h, wh) + dot(h, wl) + dot(low[...], wh))


def cost(us):
    return pl.CostEstimate(flops=int(us * 5e8), bytes_accessed=0, transcendentals=0)


def params(**kw):
    return pltpu.CompilerParams(vmem_limit_bytes=28 * 1024 * 1024, **kw)


def factor_shapes(steps, blocks):
    return (
        jax.ShapeDtypeStruct((steps, NB, blocks * NB), BF16),
        jax.ShapeDtypeStruct((steps, NB, blocks * NB), BF16),
        jax.ShapeDtypeStruct((steps, NB, NB), F32),
    )


def factor_scratch(steps, blocks):
    return [
        pltpu.VMEM((steps, NB, blocks * NB), BF16),
        pltpu.VMEM((steps, NB, blocks * NB), BF16),
        pltpu.VMEM((NB, NB), F32),
    ]


def first_factor_call(core, mine, other, ridge):
    blocks = mine.shape[0] * 4
    steps = blocks // 2
    vmem = pl.BlockSpec(memory_space=pltpu.VMEM)
    return pl.pallas_call(
        lambda *refs: first_factor_kernel(*refs, ridge=ridge),
        in_specs=[pl.BlockSpec(memory_space=pltpu.SMEM), vmem, vmem],
        out_shape=(
            *factor_shapes(steps, blocks),
            jax.ShapeDtypeStruct((blocks - steps, NB, (blocks - steps) * NB), F32),
        ),
        scratch_shapes=[
            pltpu.VMEM((blocks, NB, blocks * NB), F32),
            *factor_scratch(steps, blocks),
        ],
        compiler_params=params(),
        cost_estimate=cost(28),
        name="factor0",
    )(core, mine, other)


def second_factor_call(matrix, ridge):
    blocks = matrix.shape[0]
    return pl.pallas_call(
        lambda *refs: second_factor_kernel(*refs, ridge=ridge),
        out_shape=factor_shapes(blocks, blocks),
        scratch_shapes=factor_scratch(blocks, blocks),
        compiler_params=params(),
        cost_estimate=cost(22),
        name="factor1",
    )(matrix)


def solve_call(factors, corr):
    return pl.pallas_call(
        solve_kernel,
        out_shape=jax.ShapeDtypeStruct(corr.shape, F32),
        scratch_shapes=[pltpu.VMEM(corr.shape, BF16) for _ in range(4)],
        compiler_params=params(),
        cost_estimate=cost(12),
        name="solve",
    )(*factors, corr)


def gram_call(frames, weights, phases):
    rows = frames.shape[1]
    feat = weights.shape[1]
    blocks = feat // NB
    return pl.pallas_call(
        gram_kernel,
        out_shape=jax.ShapeDtypeStruct((blocks // 2, NB, feat + NB), F32),
        scratch_shapes=[pltpu.VMEM((rows, feat), BF16), pltpu.VMEM((rows, feat), BF16)],
        compiler_params=params(),
        cost_estimate=cost(7),
        name="gram",
    )(frames, weights, phases)


def feature_call(order, tops, bottoms, weights, phases, residual, tile=256):
    rows, cols = residual.shape
    width = tops[0].shape[1]
    feat = weights.shape[1]
    half = rows // tile // 2
    return pl.pallas_call(
        feature_kernel,
        grid=(rows // tile,),
        in_specs=[
            pl.BlockSpec(memory_space=pltpu.SMEM),
            *[pl.BlockSpec((tile, width), lambda i: (jnp.minimum(i, half - 1), 0))] * 4,
            *[pl.BlockSpec((tile, width), lambda i: (jnp.maximum(i - half, 0), 0))] * 4,
            pl.BlockSpec((4, width, feat), lambda i: (0, 0, 0)),
            pl.BlockSpec((1, feat), lambda i: (0, 0)),
            pl.BlockSpec((tile, cols), lambda i: (i, 0)),
        ],
        out_specs=[
            pl.BlockSpec((tile, feat), lambda i: (i, 0)),
            pl.BlockSpec((tile, feat), lambda i: (i, 0)),
            pl.BlockSpec((feat, cols), lambda i: (0, 0)),
        ],
        out_shape=[
            jax.ShapeDtypeStruct((rows, feat), BF16),
            jax.ShapeDtypeStruct((rows, feat), BF16),
            jax.ShapeDtypeStruct((feat, cols), F32),
        ],
        compiler_params=params(dimension_semantics=("arbitrary",)),
        cost_estimate=cost(15),
        name="features",
    )(order, *tops, *bottoms, weights.reshape(4, width, feat), phases, residual)


def update_call(high, low, coef, residual, tile=256):
    rows, feat = high.shape
    cols = residual.shape[1]
    return pl.pallas_call(
        update_kernel,
        grid=(rows // tile,),
        in_specs=[
            pl.BlockSpec((tile, feat), lambda i: (i, 0)),
            pl.BlockSpec((tile, feat), lambda i: (i, 0)),
            pl.BlockSpec((feat, cols), lambda i: (0, 0)),
            pl.BlockSpec((tile, cols), lambda i: (i, 0)),
        ],
        out_specs=pl.BlockSpec((tile, cols), lambda i: (i, 0)),
        out_shape=jax.ShapeDtypeStruct((rows, cols), F32),
        compiler_params=params(dimension_semantics=("arbitrary",)),
        cost_estimate=cost(10),
        name="update",
    )(high, low, coef, residual)


UP = [(i, (i + 1) % 4) for i in range(4)]
DOWN = [(i, (i - 1) % 4) for i in range(4)]
SWAP = [(0, 1), (1, 0)]


def exchange(parts, axes):
    return lax.all_to_all(parts, axes, 0, 0, tiled=True)


def to_everyone(value, axes):
    return exchange(jnp.broadcast_to(value[None], (lax.axis_size(axes), *value.shape)), axes)


def ring_slabs(own):
    half = own.shape[0] // 2
    top, bottom = own[:half], own[half:]
    left_top = lax.ppermute(top, "tgt", UP)
    right_bottom = lax.ppermute(bottom, "tgt", DOWN)
    left_bottom = lax.ppermute(bottom, "tgt", UP)
    right_top = lax.ppermute(top, "tgt", DOWN)
    far_top = lax.ppermute(left_top, "tgt", UP)
    far_bottom = lax.ppermute(right_bottom, "tgt", DOWN)
    return (top, left_top, right_top, far_top), (bottom, left_bottom, right_bottom, far_bottom)


def summed_gram(pack, core):
    halves = pack.reshape(2, -1, *pack.shape[1:])
    mine = lax.dynamic_index_in_dim(halves, core, 0, keepdims=False)
    other = lax.dynamic_index_in_dim(halves, 1 - core, 0, keepdims=False)
    mine = mine + lax.ppermute(other, "core", SWAP)
    chips = ("y", "z", "tgt")
    count = lax.axis_size(chips)
    parts = mine.reshape(count, -1, mine.shape[-1])
    parts = exchange(parts, chips)
    piece = jnp.sum(parts, axis=0)
    mine = to_everyone(piece, chips).reshape(mine.shape)
    return mine, lax.ppermute(mine, "core", SWAP)


def summed_corr(corr):
    plane = ("y", "z")
    count = lax.axis_size(plane)
    parts = exchange(corr.reshape(count, -1, corr.shape[-1]), plane)
    piece = jnp.sum(parts, axis=0)
    piece = piece + lax.ppermute(piece, "core", SWAP)
    return to_everyone(piece, plane).reshape(corr.shape)


def block_step(frames, weights, phases, residual):
    rows_here = frames.shape[0]
    feature_count = weights.shape[1]
    ridge = 0.1 * rows_here * lax.axis_size(("y", "z", "core")) / feature_count
    phases = phases[None, :]
    core = lax.axis_index("core")
    at = lax.axis_index("tgt")
    whole_rows = exchange(frames.reshape(4, rows_here // 4, -1), "tgt")
    whole_rows, own = lax.optimization_barrier((whole_rows, frames))
    tops, bottoms = ring_slabs(own)
    pack = gram_call(whole_rows, weights, phases)
    mine, other = summed_gram(pack, core)
    order = jnp.stack([at, at + 3, at + 1, at + 2]) % 4
    high, low, corr = feature_call(order, tops, bottoms, weights, phases, residual)
    corr = summed_corr(corr)
    *factor0, rest = first_factor_call(core[None], mine, other, ridge)
    factor1 = second_factor_call(rest, ridge)
    coefficients = solve_call((*factor0, *factor1), corr)
    residual_next = update_call(high, low, coefficients, residual)
    return (residual_next, coefficients)


def solution(mesh):
    rows = ("y", "z", "core")
    mesh = jax.sharding.Mesh(mesh.devices.reshape(4, 4, 2, 4), (*rows, "tgt"))
    return jax.shard_map(
        block_step,
        mesh=mesh,
        in_specs=(P(rows, "tgt"), P(), P(), P(rows, "tgt")),
        out_specs=(P(rows, "tgt"), P(None, "tgt")),
        check_vma=False,
    )
```

profile of v0, /device:TPU:1, one launch (start us, length us, event | category | flops | bytes accessed | tf_op | source)
XLA Modules:
  0.0 199.6 jit_solution(11550048295578391187)
XLA Ops:
  0.6 4.8 %all-to-all-start = ((bf16[4,512,128]{2,1,0:T(8,128)(2,1)}), bf16[4,512,128]{2,1,0:T(8,128)(2,1)S(1)}, u32[]{:S(2)}, u32[]{:S(2)}) async-start(bf16[4,512,128]{2,1,0:T(8,128)(2,1)} %bitcast.22), calls=%async_computation | async-start | bytes 1048576 | tf_op jit(solution)/shard_map/all_to_all | solution.py:387
  5.5 8.3 %all-to-all-done.frames = bf16[4,512,128]{2,1,0:T(8,128)(2,1)S(1)} async-done(((bf16[4,512,128]{2,1,0:T(8,128)(2,1)}), bf16[4,512,128]{2,1,0:T(8,128)(2,1)S(1)}, u32[]{:S(2)}, u32[]{:S(2)}) %all-to-all-start) | async-done | bytes 524320 | tf_op jit(solution)/shard_map/all_to_all | solution.py:387
  13.8 1.2 copy-done.2
  15.0 0.7 copy-done.4
  15.7 4.2 %gram.1 = f32[4,128,1152]{2,1,0:T(8,128)S(1)} custom-call(bf16[4,512,128]{2,1,0:T(8,128)(2,1)S(1)} %all-to-all-done.frames, bf16[512,1024]{1,0:T(8,128)(2,1)S(1)} %copy-done.2, f32[1,1024]{1,0:T(1,128)S(1)} %bitcast.20), custom_call_target="tpu_custom_call" | custom-call | flops 3500000000 | tf_op jit(solution)/shard_map/gram/pallas_call | solution.py:319
  19.9 0.1 dynamic-slice_bitcast_fusion
  20.0 2.2 %collective-permute-start.6 = (f32[2,128,1152]{2,1,0:T(8,128)S(1)}, f32[2,128,1152]{2,1,0:T(8,128)}, u32[]{:S(2)}, u32[]{:S(2)}) collective-permute-start(f32[2,128,1152]{2,1,0:T(8,128)S(1)} %dynamic-slice_bitcast_fusion), channel_id=1, source_target_pairs={{0,4},{4,0},{1,5},{5,1},{2,6},{6,2},{3,7},{7,3},{8,12},{12,8},{9,1... | collective-permute-start | bytes 3538952 | tf_op jit(solution)/shard_map/ppermute | solution.py:410
  22.2 2.6 %collective-permute-done.6 = f32[2,128,1152]{2,1,0:T(8,128)} collective-permute-done((f32[2,128,1152]{2,1,0:T(8,128)S(1)}, f32[2,128,1152]{2,1,0:T(8,128)}, u32[]{:S(2)}, u32[]{:S(2)}) %collective-permute-start.6) | collective-permute-done | bytes 1179680 | tf_op jit(solution)/shard_map/ppermute | solution.py:410
  24.8 1.4 bitcast_add_fusion
  26.2 0.3 reshape.30
  26.6 28.7 %all_to_all.25 = f32[64,4,1152]{2,1,0:T(4,128)S(1)} all-to-all(f32[64,4,1152]{2,1,0:T(4,128)S(1)} %reshape.30), channel_id=1, replica_groups=mesh['y'=4,'z'=4,'core'=2,'tgt'=4] {'y','z','tgt'}, dimensions={0} | all-to-all | bytes 2359296 | tf_op jit(solution)/shard_map/all_to_all | solution.py:387
  55.3 0.2 reduce_sum.18
  55.5 1.2 broadcast_in_dim.20
  56.6 4.8 %all-to-all-start.2 = ((f32[64,4,1152]{2,1,0:T(4,128)}), f32[64,4,1152]{2,1,0:T(4,128)S(1)}, u32[]{:S(2)}, u32[]{:S(2)}) async-start(f32[64,4,1152]{2,1,0:T(4,128)} %broadcast_in_dim.20), calls=%async_computation.2 | async-start | bytes 2359296 | tf_op jit(solution)/shard_map/all_to_all | solution.py:387
  61.4 0.0 copy-done.23
  61.5 2.2 %collective-permute-start.4 = (bf16[1024,128]{1,0:T(8,128)(2,1)S(1)}, bf16[1024,128]{1,0:T(8,128)(2,1)S(1)}, u32[]{:S(2)}, u32[]{:S(2)}) collective-permute-start(bf16[1024,128]{1,0:T(8,128)(2,1)S(1)} %get-tuple-element.26.refs_4_), channel_id=1, source_target_pairs={{0,3},{1,0},{2,1},{3,2},{4,7},{5,4},{6,5},{7,6},{8,11},{9,8},{10,9... | collective-permute-start | bytes 786440 | tf_op jit(solution)/shard_map/ppermute | solution.py:398
  63.7 0.0 collective-permute-start
  63.7 0.2 collective-permute-start.3
  63.9 2.5 %collective-permute-start.1 = (bf16[1024,128]{1,0:T(8,128)(2,1)S(1)}, bf16[1024,128]{1,0:T(8,128)(2,1)}, u32[]{:S(2)}, u32[]{:S(2)}) collective-permute-start(bf16[1024,128]{1,0:T(8,128)(2,1)S(1)} %get-tuple-element.27.refs_0_), channel_id=1, source_target_pairs={{0,3},{1,0},{2,1},{3,2},{4,7},{5,4},{6,5},{7,6},{8,11},{9,8},{10,9... | collective-permute-start | bytes 786440 | tf_op jit(solution)/shard_map/ppermute | solution.py:400
  66.4 13.2 %collective-permute-done.4.refs_6_ = bf16[1024,128]{1,0:T(8,128)(2,1)S(1)} collective-permute-done((bf16[1024,128]{1,0:T(8,128)(2,1)S(1)}, bf16[1024,128]{1,0:T(8,128)(2,1)S(1)}, u32[]{:S(2)}, u32[]{:S(2)}) %collective-permute-start.4) | collective-permute-done | bytes 262176 | tf_op jit(solution)/shard_map/ppermute | solution.py:398
  79.6 2.4 %collective-permute-start.5 = (bf16[1024,128]{1,0:T(8,128)(2,1)S(1)}, bf16[1024,128]{1,0:T(8,128)(2,1)}, u32[]{:S(2)}, u32[]{:S(2)}) collective-permute-start(bf16[1024,128]{1,0:T(8,128)(2,1)S(1)} %collective-permute-done.4.refs_6_), channel_id=1, source_target_pairs={{0,3},{1,0},{2,1},{3,2},{4,7},{5,4},{6,5},{7,6},{8,11},{9,8},{10,9... | collective-permute-start | bytes 786440 | tf_op jit(solution)/shard_map/ppermute | solution.py:402
  82.0 0.0 collective-permute-done.refs_1_
  82.0 0.0 collective-permute-start.2
  82.0 0.1 and_select_fusion.order
  82.1 0.0 all-to-all-done.2
  82.1 0.4 reshape.31.refs_1_
  82.5 4.5 %collective-permute-start.7 = (f32[2,128,1152]{2,1,0:T(8,128)S(1)}, f32[2,128,1152]{2,1,0:T(8,128)S(1)}, u32[]{:S(2)}, u32[]{:S(2)}) collective-permute-start(f32[2,128,1152]{2,1,0:T(8,128)S(1)} %reshape.31.refs_1_), channel_id=1, source_target_pairs={{0,4},{4,0},{1,5},{5,1},{2,6},{6,2},{3,7},{7,3},{8,12},{12,8},{9,1... | collective-permute-start | bytes 3538952 | tf_op jit(solution)/shard_map/ppermute | solution.py:417
  87.0 0.4 collective-permute-done.3.refs_5_
  87.4 0.0 collective-permute-done.1.refs_2_
  87.4 3.4 %collective-permute-done.5.refs_7_ = bf16[1024,128]{1,0:T(8,128)(2,1)} collective-permute-done((bf16[1024,128]{1,0:T(8,128)(2,1)S(1)}, bf16[1024,128]{1,0:T(8,128)(2,1)}, u32[]{:S(2)}, u32[]{:S(2)}) %collective-permute-start.5) | collective-permute-done | bytes 262176 | tf_op jit(solution)/shard_map/ppermute | solution.py:402
  90.8 2.0 %collective-permute-done.2.refs_3_ = bf16[1024,128]{1,0:T(8,128)(2,1)} collective-permute-done((bf16[1024,128]{1,0:T(8,128)(2,1)}, bf16[1024,128]{1,0:T(8,128)(2,1)}, u32[]{:S(2)}, u32[]{:S(2)}) %collective-permute-start.2) | collective-permute-done | bytes 262176 | tf_op jit(solution)/shard_map/ppermute | solution.py:401
  92.9 0.0 copy-done.5
  92.9 1.6 copy-done
  94.5 1.2 copy-done.3
  95.7 14.4 %features.1 = (bf16[2048,1024]{1,0:T(8,128)(2,1)S(1)}, bf16[2048,1024]{1,0:T(8,128)(2,1)S(1)}, f32[1024,256]{1,0:T(8,128)S(1)}) custom-call(s32[4]{0:T(128)S(1)} %and_select_fusion.order, bf16[1024,128]{1,0:T(8,128)(2,1)S(1)} %get-tuple-element.27.refs_0_, bf16[1024,128]{1,0:T(8,128)(2,1)} %collective-permute-done.refs_1_, ...), custom_call_target="tpu_custom_call" | custom-call | flops 7500000256 | tf_op jit(solution)/shard_map/features/pallas_call | solution.py:334
  110.1 0.0 copy-start.7
  110.1 2.0 copy-done.7
  112.1 2.0 %copy-done.9 = bf16[2048,1024]{1,0:T(8,128)(2,1)} copy-done((bf16[2048,1024]{1,0:T(8,128)(2,1)}, bf16[2048,1024]{1,0:T(8,128)(2,1)S(1)}, u32[]{:S(2)}) %copy-start.9) | copy-done | bytes 4194328
  114.1 21.5 %all_to_all.26 = f32[16,64,256]{2,1,0:T(8,128)S(1)} all-to-all(f32[16,64,256]{2,1,0:T(8,128)S(1)} %bitcast.18), channel_id=1, replica_groups=mesh['y'=4,'z'=4,'core'=2,'tgt'=4] {'y','z'}, dimensions={0} | all-to-all | bytes 2097152 | tf_op jit(solution)/shard_map/all_to_all | solution.py:387
  135.6 0.1 reduce_sum.19
  135.7 3.1 %collective-permute-start.8 = (f32[64,256]{1,0:T(8,128)S(1)}, f32[64,256]{1,0:T(8,128)S(1)}, u32[]{:S(2)}, u32[]{:S(2)}) collective-permute-start(f32[64,256]{1,0:T(8,128)S(1)} %reduce_sum.19), channel_id=1, source_target_pairs={{0,4},{4,0},{1,5},{5,1},{2,6},{6,2},{3,7},{7,3},{8,12},{12,8},{9,1... | collective-permute-start | bytes 196616 | tf_op jit(solution)/shard_map/ppermute | solution.py:425
  138.8 0.9 collective-permute-done.8
  139.7 1.1 broadcast_in_dim.21
  140.8 3.7 %all-to-all-start.4 = ((f32[16,64,256]{2,1,0:T(8,128)}), f32[16,64,256]{2,1,0:T(8,128)S(1)}, u32[]{:S(2)}, u32[]{:S(2)}) async-start(f32[16,64,256]{2,1,0:T(8,128)} %broadcast_in_dim.21), calls=%async_computation.4 | async-start | bytes 2097152 | tf_op jit(solution)/shard_map/all_to_all | solution.py:387
  144.5 0.0 collective-permute-done.7.refs_2_
  144.5 18.7 %factor0.1 = (bf16[4,128,1024]{2,1,0:T(8,128)(2,1)S(1)}, bf16[4,128,1024]{2,1,0:T(8,128)(2,1)S(1)}, f32[4,128,128]{2,1,0:T(8,128)S(1)}, f32[4,128,512]{2,1,0:T(8,128)S(1)}) custom-call(s32[1]{0:T(128)} %bitcast.7.refs_0_, f32[2,128,1152]{2,1,0:T(8,128)S(1)} %reshape.31.refs_1_, f32[2,128,1152]{2,1,0:T(8,128)S(1)} %collective-permute-done.7.refs_2_), custom_call_target="tpu_custom_call" | custom-call | flops 14000000000 | tf_op jit(solution)/shard_map/factor0/pallas_call | solution.py:275
  163.2 0.0 copy-start.11
  163.2 1.0 copy-done.11
  164.1 1.0 copy-done.13
  165.1 0.7 copy-done.19
  165.8 15.9 %factor1.1 = (bf16[4,128,512]{2,1,0:T(8,128)(2,1)S(1)}, bf16[4,128,512]{2,1,0:T(8,128)(2,1)S(1)}, f32[4,128,128]{2,1,0:T(8,128)S(1)}) custom-call(f32[4,128,512]{2,1,0:T(8,128)S(1)} %get-tuple-element.21.refs_0_), custom_call_target="tpu_custom_call" | custom-call | flops 11000000512 | tf_op jit(solution)/shard_map/factor1/pallas_call | solution.py:294
  181.8 0.0 copy-start.15
  181.8 0.8 copy-done.15
  182.5 0.8 copy-done.17
  183.4 0.7 copy-done.21
  184.1 0.0 all-to-all-done.4
  184.1 0.0 copy-done.12
  184.1 1.0 copy-done.16
  185.1 1.0 copy-done.18
  186.2 0.9 copy-done.22
  187.1 5.5 %solve.1.coef = f32[1024,256]{1,0:T(8,128)} custom-call(bf16[4,128,1024]{2,1,0:T(8,128)(2,1)S(1)} %copy-done.12, bf16[4,128,1024]{2,1,0:T(8,128)(2,1)S(1)} %copy-done.14, f32[4,128,128]{2,1,0:T(8,128)S(1)} %copy-done.20, bf16[4,128,512]{2,1,0:T(8,128)(2,1)S(1)} %copy-done.16, bf16[4,128,512]{2,1,0:T(8,128)(2,1)S(1)} %copy-done.18, ...), custom_call_target="tpu_custom_call" | custom-call | flops 6000000000 | tf_op jit(solution)/shard_map/solve/pallas_call | solution.py:305
  192.7 0.0 copy-done.10
  192.7 1.2 copy-done.6
  193.9 5.7 %update.1 = f32[2048,256]{1,0:T(8,128)} custom-call(bf16[2048,1024]{1,0:T(8,128)(2,1)S(1)} %copy-done.8, bf16[2048,1024]{1,0:T(8,128)(2,1)S(1)} %copy-done.10, f32[1024,256]{1,0:T(8,128)S(1)} %copy-done.6, f32[2048,256]{1,0:T(8,128)S(1)} %copy-done.1), custom_call_target="tpu_custom_call" | custom-call | flops 5000000000 | tf_op jit(solution)/shard_map/update/pallas_call | solution.py:364
  (27 shorter events, 0.1 us)
Async XLA Ops:
  0.6 13.2 %all-to-all-start = ((bf16[4,512,128]{2,1,0:T(8,128)(2,1)}), bf16[4,512,128]{2,1,0:T(8,128)(2,1)S(1)}, u32[]{:S(2)}, u32[]{:S(2)}) async-start(bf16[4,512,128]{2,1,0:T(8,128)(2,1)} %bitcast.22), calls=%async_computation | async-start | bytes 1048576 | tf_op jit(solution)/shard_map/all_to_all | solution.py:387
  13.8 1.2 copy-start.2
  15.0 0.7 copy-start.4
  20.0 4.8 %collective-permute-start.6 = (f32[2,128,1152]{2,1,0:T(8,128)S(1)}, f32[2,128,1152]{2,1,0:T(8,128)}, u32[]{:S(2)}, u32[]{:S(2)}) collective-permute-start(f32[2,128,1152]{2,1,0:T(8,128)S(1)} %dynamic-slice_bitcast_fusion), channel_id=1, source_target_pairs={{0,4},{4,0},{1,5},{5,1},{2,6},{6,2},{3,7},{7,3},{8,12},{12,8},{9,1... | collective-permute-start | bytes 3538952 | tf_op jit(solution)/shard_map/ppermute | solution.py:410
  56.6 4.8 %copy-start.23 = (bf16[2048,128]{1,0:T(8,128)(2,1)S(1)}, bf16[2048,128]{1,0:T(8,128)(2,1)}, u32[]{:S(2)}) copy-start(bf16[2048,128]{1,0:T(8,128)(2,1)} %param.4) | copy-start | bytes 1572868
  56.6 25.5 %all-to-all-start.2 = ((f32[64,4,1152]{2,1,0:T(4,128)}), f32[64,4,1152]{2,1,0:T(4,128)S(1)}, u32[]{:S(2)}, u32[]{:S(2)}) async-start(f32[64,4,1152]{2,1,0:T(4,128)} %broadcast_in_dim.20), calls=%async_computation.2 | async-start | bytes 2359296 | tf_op jit(solution)/shard_map/all_to_all | solution.py:387
  61.5 18.1 %collective-permute-start.4 = (bf16[1024,128]{1,0:T(8,128)(2,1)S(1)}, bf16[1024,128]{1,0:T(8,128)(2,1)S(1)}, u32[]{:S(2)}, u32[]{:S(2)}) collective-permute-start(bf16[1024,128]{1,0:T(8,128)(2,1)S(1)} %get-tuple-element.26.refs_4_), channel_id=1, source_target_pairs={{0,3},{1,0},{2,1},{3,2},{4,7},{5,4},{6,5},{7,6},{8,11},{9,8},{10,9... | collective-permute-start | bytes 786440 | tf_op jit(solution)/shard_map/ppermute | solution.py:398
  63.7 18.4 %collective-permute-start = (bf16[1024,128]{1,0:T(8,128)(2,1)S(1)}, bf16[1024,128]{1,0:T(8,128)(2,1)}, u32[]{:S(2)}, u32[]{:S(2)}) collective-permute-start(bf16[1024,128]{1,0:T(8,128)(2,1)S(1)} %get-tuple-element.27.refs_0_), channel_id=1, source_target_pairs={{0,1},{1,2},{2,3},{3,0},{4,5},{5,6},{6,7},{7,4},{8,9},{9,10},{10,1... | collective-permute-start | bytes 786440 | tf_op jit(solution)/shard_map/ppermute | solution.py:397
  63.7 23.8 %collective-permute-start.3 = (bf16[1024,128]{1,0:T(8,128)(2,1)S(1)}, bf16[1024,128]{1,0:T(8,128)(2,1)}, u32[]{:S(2)}, u32[]{:S(2)}) collective-permute-start(bf16[1024,128]{1,0:T(8,128)(2,1)S(1)} %get-tuple-element.26.refs_4_), channel_id=1, source_target_pairs={{0,1},{1,2},{2,3},{3,0},{4,5},{5,6},{6,7},{7,4},{8,9},{9,10},{10,1... | collective-permute-start | bytes 786440 | tf_op jit(solution)/shard_map/ppermute | solution.py:399
  63.9 23.5 %collective-permute-start.1 = (bf16[1024,128]{1,0:T(8,128)(2,1)S(1)}, bf16[1024,128]{1,0:T(8,128)(2,1)}, u32[]{:S(2)}, u32[]{:S(2)}) collective-permute-start(bf16[1024,128]{1,0:T(8,128)(2,1)S(1)} %get-tuple-element.27.refs_0_), channel_id=1, source_target_pairs={{0,3},{1,0},{2,1},{3,2},{4,7},{5,4},{6,5},{7,6},{8,11},{9,8},{10,9... | collective-permute-start | bytes 786440 | tf_op jit(solution)/shard_map/ppermute | solution.py:400
  79.6 11.2 %collective-permute-start.5 = (bf16[1024,128]{1,0:T(8,128)(2,1)S(1)}, bf16[1024,128]{1,0:T(8,128)(2,1)}, u32[]{:S(2)}, u32[]{:S(2)}) collective-permute-start(bf16[1024,128]{1,0:T(8,128)(2,1)S(1)} %collective-permute-done.4.refs_6_), channel_id=1, source_target_pairs={{0,3},{1,0},{2,1},{3,2},{4,7},{5,4},{6,5},{7,6},{8,11},{9,8},{10,9... | collective-permute-start | bytes 786440 | tf_op jit(solution)/shard_map/ppermute | solution.py:402
  82.0 10.8 %collective-permute-start.2 = (bf16[1024,128]{1,0:T(8,128)(2,1)}, bf16[1024,128]{1,0:T(8,128)(2,1)}, u32[]{:S(2)}, u32[]{:S(2)}) collective-permute-start(bf16[1024,128]{1,0:T(8,128)(2,1)} %collective-permute-done.refs_1_), channel_id=1, source_target_pairs={{0,1},{1,2},{2,3},{3,0},{4,5},{5,6},{6,7},{7,4},{8,9},{9,10},{10,1... | collective-permute-start | bytes 786440 | tf_op jit(solution)/shard_map/ppermute | solution.py:401
  82.1 10.8 %copy-start.5 = (f32[1024]{0:T(1024)S(1)}, f32[1024]{0:T(1024)}, u32[]{:S(2)}) copy-start(f32[1024]{0:T(1024)} %param.6) | copy-start | bytes 12292
  82.5 61.9 %collective-permute-start.7 = (f32[2,128,1152]{2,1,0:T(8,128)S(1)}, f32[2,128,1152]{2,1,0:T(8,128)S(1)}, u32[]{:S(2)}, u32[]{:S(2)}) collective-permute-start(f32[2,128,1152]{2,1,0:T(8,128)S(1)} %reshape.31.refs_1_), channel_id=1, source_target_pairs={{0,4},{4,0},{1,5},{5,1},{2,6},{6,2},{3,7},{7,3},{8,12},{12,8},{9,1... | collective-permute-start | bytes 3538952 | tf_op jit(solution)/shard_map/ppermute | solution.py:417
  92.9 1.6 copy-start
  94.5 1.2 copy-start.3
  110.1 2.0 copy-start.7
  112.1 2.0 %copy-start.9 = (bf16[2048,1024]{1,0:T(8,128)(2,1)}, bf16[2048,1024]{1,0:T(8,128)(2,1)S(1)}, u32[]{:S(2)}) copy-start(bf16[2048,1024]{1,0:T(8,128)(2,1)S(1)} %get-tuple-element.16.low) | copy-start | bytes 12582916
  135.7 4.0 %collective-permute-start.8 = (f32[64,256]{1,0:T(8,128)S(1)}, f32[64,256]{1,0:T(8,128)S(1)}, u32[]{:S(2)}, u32[]{:S(2)}) collective-permute-start(f32[64,256]{1,0:T(8,128)S(1)} %reduce_sum.19), channel_id=1, source_target_pairs={{0,4},{4,0},{1,5},{5,1},{2,6},{6,2},{3,7},{7,3},{8,12},{12,8},{9,1... | collective-permute-start | bytes 196616 | tf_op jit(solution)/shard_map/ppermute | solution.py:425
  140.8 43.2 %all-to-all-start.4 = ((f32[16,64,256]{2,1,0:T(8,128)}), f32[16,64,256]{2,1,0:T(8,128)S(1)}, u32[]{:S(2)}, u32[]{:S(2)}) async-start(f32[16,64,256]{2,1,0:T(8,128)} %broadcast_in_dim.21), calls=%async_computation.4 | async-start | bytes 2097152 | tf_op jit(solution)/shard_map/all_to_all | solution.py:387
  163.2 1.0 copy-start.11
  164.1 1.0 copy-start.13
  165.1 0.7 copy-start.19
  165.8 18.3 %copy-start.12 = (bf16[4,128,1024]{2,1,0:T(8,128)(2,1)S(1)}, bf16[4,128,1024]{2,1,0:T(8,128)(2,1)}, u32[]{:S(2)}) copy-start(bf16[4,128,1024]{2,1,0:T(8,128)(2,1)} %copy-done.11) | copy-start | bytes 3145732
  165.8 18.3 %copy-start.14 = (bf16[4,128,1024]{2,1,0:T(8,128)(2,1)S(1)}, bf16[4,128,1024]{2,1,0:T(8,128)(2,1)}, u32[]{:S(2)}) copy-start(bf16[4,128,1024]{2,1,0:T(8,128)(2,1)} %copy-done.13) | copy-start | bytes 3145732
  165.8 18.3 %copy-start.20 = (f32[4,128,128]{2,1,0:T(8,128)S(1)}, f32[4,128,128]{2,1,0:T(8,128)}, u32[]{:S(2)}) copy-start(f32[4,128,128]{2,1,0:T(8,128)} %copy-done.19) | copy-start | bytes 786436
  181.8 0.8 copy-start.15
  182.5 0.8 copy-start.17
  183.4 0.7 copy-start.21
  184.1 1.0 copy-start.16
  185.1 1.0 copy-start.18
  186.2 0.9 copy-start.22
  187.1 5.5 %copy-start.1 = (f32[2048,256]{1,0:T(8,128)S(1)}, f32[2048,256]{1,0:T(8,128)}, u32[]{:S(2)}) copy-start(f32[2048,256]{1,0:T(8,128)} %residual.1) | copy-start | bytes 6291460
  187.1 5.5 %copy-start.8 = (bf16[2048,1024]{1,0:T(8,128)(2,1)S(1)}, bf16[2048,1024]{1,0:T(8,128)(2,1)}, u32[]{:S(2)}) copy-start(bf16[2048,1024]{1,0:T(8,128)(2,1)} %copy-done.7) | copy-start | bytes 12582916
  187.1 5.5 %copy-start.10 = (bf16[2048,1024]{1,0:T(8,128)(2,1)S(1)}, bf16[2048,1024]{1,0:T(8,128)(2,1)}, u32[]{:S(2)}) copy-start(bf16[2048,1024]{1,0:T(8,128)(2,1)} %copy-done.9) | copy-start | bytes 12582916
  192.7 1.2 copy-start.6
where the time goes:
time: 200 us
  Pallas kernels  64.5 us (32%)
  blocking collectives  50.2 us (25%)
  waiting for transfers between devices  30.9 us (15%)
  starting transfers between devices  30.4 us (15%)
  local copies, waits for them, and re-layouts  21.1 us (11%)
    all_to_all x2, blocking collectives, exchange(): return lax.all_to_all(parts, axes, 0, 0, tiled=True)  50.2 us
    pallas_call x1, Pallas kernels, first_factor_call(): pl.pallas_call(lambda *refs: first_factor_kernel(*refs, ridge=ridge), in_...  18.7 us
    unnamed x48, local copies, waits for them, and re-layouts  17.9 us
    pallas_call x1, Pallas kernels, second_factor_call(): pl.pallas_call(lambda *refs: second_factor_kernel(*refs, ridge=ridge), ou...  15.9 us
    pallas_call x1, Pallas kernels, feature_call(): pl.pallas_call(feature_kernel, grid=(rows // tile,), in_specs=[pl.BlockSp...  14.4 us
    all_to_all x3, starting transfers between devices, exchange(): return lax.all_to_all(parts, axes, 0, 0, tiled=True)  13.3 us
    ppermute x1, waiting for transfers between devices, ring_slabs(): right_bottom = lax.ppermute(bottom, 'tgt', DOWN)  13.2 us
    all_to_all x3, waiting for transfers between devices, exchange(): return lax.all_to_all(parts, axes, 0, 0, tiled=True)  8.33 us
  transfers between devices with their start and end apart: 12, of which 7 were waited for; matrix products, arithmetic and copies ran while one was open for 1% of the time, Pallas kernels for 25%

commit v1 on v0

--- a/solution.py
+++ b/solution.py
@@ -73,8 +73,9 @@
     return blocks - 1 - block, (block + 1) * NB
 
 
-def gram_kernel(frames, weights, phases, out, high, low):
-    blocks = out.shape[0] * 2
+def gram_kernel(core, frames, weights, phases, mine, other, high, low):
+    quarter = mine.shape[0]
+    blocks = quarter * 4
     slabs = jnp.concatenate([frames[i] for i in range(frames.shape[0])], axis=1)
     h, l = split2(features(slabs, weights[...], phases[...]))
     high[...] = h
@@ -86,7 +87,13 @@
         g = g + dot_t(high[:, rows], low[:, right])
         g = g + dot_t(low[:, rows], high[:, right])
         at, col = packed_slot(i, blocks)
-        out[at, :, col : col + (blocks - i) * NB] = g
+        own = core[0] == at // quarter
+
+        def store(half):
+            half[at % quarter, :, col : col + (blocks - i) * NB] = g
+
+        pl.when(own)(lambda: store(mine))
+        pl.when(jnp.logical_not(own))(lambda: store(other))
 
 
 def feature_kernel(order, *refs):
@@ -248,8 +255,8 @@
     return pl.CostEstimate(flops=int(us * 5e8), bytes_accessed=0, transcendentals=0)
 
 
-def params(**kw):
-    return pltpu.CompilerParams(vmem_limit_bytes=28 * 1024 * 1024, **kw)
+def params(mib, **kw):
+    return pltpu.CompilerParams(vmem_limit_bytes=mib * 1024 * 1024, **kw)
 
 
 def factor_shapes(steps, blocks):
@@ -283,7 +290,7 @@
             pltpu.VMEM((blocks, NB, blocks * NB), F32),
             *factor_scratch(steps, blocks),
         ],
-        compiler_params=params(),
+        compiler_params=params(56),
         cost_estimate=cost(28),
         name="factor0",
     )(core, mine, other)
@@ -295,7 +302,7 @@
         lambda *refs: second_factor_kernel(*refs, ridge=ridge),
         out_shape=factor_shapes(blocks, blocks),
         scratch_shapes=factor_scratch(blocks, blocks),
-        compiler_params=params(),
+        compiler_params=params(56),
         cost_estimate=cost(22),
         name="factor1",
     )(matrix)
@@ -306,24 +313,26 @@
         solve_kernel,
         out_shape=jax.ShapeDtypeStruct(corr.shape, F32),
         scratch_shapes=[pltpu.VMEM(corr.shape, BF16) for _ in range(4)],
-        compiler_params=params(),
+        compiler_params=params(28),
         cost_estimate=cost(12),
         name="solve",
     )(*factors, corr)
 
 
-def gram_call(frames, weights, phases):
+def gram_call(core, frames, weights, phases):
     rows = frames.shape[1]
     feat = weights.shape[1]
-    blocks = feat // NB
+    vmem = pl.BlockSpec(memory_space=pltpu.VMEM)
+    half = jax.ShapeDtypeStruct((feat // NB // 4, NB, feat + NB), F32)
     return pl.pallas_call(
         gram_kernel,
-        out_shape=jax.ShapeDtypeStruct((blocks // 2, NB, feat + NB), F32),
+        in_specs=[pl.BlockSpec(memory_space=pltpu.SMEM), vmem, vmem, vmem],
+        out_shape=(half, half),
         scratch_shapes=[pltpu.VMEM((rows, feat), BF16), pltpu.VMEM((rows, feat), BF16)],
-        compiler_params=params(),
+        compiler_params=params(28),
         cost_estimate=cost(7),
         name="gram",
-    )(frames, weights, phases)
+    )(core, frames, weights, phases)
 
 
 def feature_call(order, tops, bottoms, weights, phases, residual, tile=256):
@@ -352,7 +361,7 @@
             jax.ShapeDtypeStruct((rows, feat), BF16),
             jax.ShapeDtypeStruct((feat, cols), F32),
         ],
-        compiler_params=params(dimension_semantics=("arbitrary",)),
+        compiler_params=params(56, dimension_semantics=("arbitrary",)),
         cost_estimate=cost(15),
         name="features",
     )(order, *tops, *bottoms, weights.reshape(4, width, feat), phases, residual)
@@ -372,7 +381,7 @@
         ],
         out_specs=pl.BlockSpec((tile, cols), lambda i: (i, 0)),
         out_shape=jax.ShapeDtypeStruct((rows, cols), F32),
-        compiler_params=params(dimension_semantics=("arbitrary",)),
+        compiler_params=params(28, dimension_semantics=("arbitrary",)),
         cost_estimate=cost(10),
         name="update",
     )(high, low, coef, residual)
@@ -403,10 +412,7 @@
     return (top, left_top, right_top, far_top), (bottom, left_bottom, right_bottom, far_bottom)
 
 
-def summed_gram(pack, core):
-    halves = pack.reshape(2, -1, *pack.shape[1:])
-    mine = lax.dynamic_index_in_dim(halves, core, 0, keepdims=False)
-    other = lax.dynamic_index_in_dim(halves, 1 - core, 0, keepdims=False)
+def summed_gram(mine, other):
     mine = mine + lax.ppermute(other, "core", SWAP)
     chips = ("y", "z", "tgt")
     count = lax.axis_size(chips)
@@ -436,8 +442,8 @@
     whole_rows = exchange(frames.reshape(4, rows_here // 4, -1), "tgt")
     whole_rows, own = lax.optimization_barrier((whole_rows, frames))
     tops, bottoms = ring_slabs(own)
-    pack = gram_call(whole_rows, weights, phases)
-    mine, other = summed_gram(pack, core)
+    halves = gram_call(core[None], whole_rows, weights, phases)
+    mine, other = summed_gram(*halves)
     order = jnp.stack([at, at + 3, at + 1, at + 2]) % 4
     high, low, corr = feature_call(order, tops, bottoms, weights, phases, residual)
     corr = summed_corr(corr)

time: 200 us -> 197 us (0.985)
  local copies, waits for them, and re-layouts: 21.1 us -> 9.25 us
  Pallas kernels: 64.5 us -> 73.7 us
    unnamed x48 -> x36, local copies, waits for them, and re-layouts: 17.9 us -> 6.21 us
    pallas_call x1, Pallas kernels: 18.7 us -> 21.3 us  [first_factor_call(): pl.pallas_call(lambda *refs: first_factor_kernel(*refs, ridge=ridge), in_...]
    pallas_call x1, Pallas kernels: 15.9 us -> 18.4 us  [second_factor_call(): pl.pallas_call(lambda *refs: second_factor_kernel(*refs, ridge=ridge), ou...]
    pallas_call x1, Pallas kernels: 4.21 us -> 6.32 us  [gram_call(): pl.pallas_call(gram_kernel, in_specs=[pl.BlockSpec(memory_space=pltpu.SME...]
    pallas_call x1, Pallas kernels: 14.4 us -> 16.5 us  [feature_call(): pl.pallas_call(feature_kernel, grid=(rows // tile,), in_specs=[pl.BlockSp...]
  transfers between devices with their start and end apart: 12 -> 12, of which waited for: 7 -> 6; matrix products, arithmetic and copies ran while one was open for 1% -> 1% of each run, Pallas kernels for 25% -> 29%
where the time goes in v1:
time: 197 us; the launch traced here: 196 us
  Pallas kernels  73.7 us (37%)
  blocking collectives  50.3 us (26%)
  starting transfers between devices  30.6 us (16%)
  waiting for transfers between devices  30.3 us (15%)
  local copies, waits for them, and re-layouts  9.25 us (5%)
    all_to_all x2, blocking collectives, exchange(): return lax.all_to_all(parts, axes, 0, 0, tiled=True)  50.3 us
    pallas_call x1, Pallas kernels, first_factor_call(): pl.pallas_call(lambda *refs: first_factor_kernel(*refs, ridge=ridge), in_...  21.3 us
    pallas_call x1, Pallas kernels, second_factor_call(): pl.pallas_call(lambda *refs: second_factor_kernel(*refs, ridge=ridge), ou...  18.4 us
    pallas_call x1, Pallas kernels, feature_call(): pl.pallas_call(feature_kernel, grid=(rows // tile,), in_specs=[pl.BlockSp...  16.5 us
    all_to_all x3, starting transfers between devices, exchange(): return lax.all_to_all(parts, axes, 0, 0, tiled=True)  13.3 us
    ppermute x1, waiting for transfers between devices, ring_slabs(): right_bottom = lax.ppermute(bottom, 'tgt', DOWN)  13.1 us
    all_to_all x3, waiting for transfers between devices, exchange(): return lax.all_to_all(parts, axes, 0, 0, tiled=True)  8.33 us
    pallas_call x1, Pallas kernels, gram_call(): pl.pallas_call(gram_kernel, in_specs=[pl.BlockSpec(memory_space=pltpu.SME...  6.32 us
  transfers between devices with their start and end apart: 12, of which 6 were waited for; matrix products, arithmetic and copies ran while one was open for 1% of the time, Pallas kernels for 29%

profile of v1, /device:TPU:1, one launch (start us, length us, event | category | flops | bytes accessed | tf_op | source)
XLA Modules:
  0.0 196.1 jit_solution(6216152555396292210)
XLA Ops:
  0.6 4.8 %all-to-all-start = ((bf16[4,512,128]{2,1,0:T(8,128)(2,1)}), bf16[4,512,128]{2,1,0:T(8,128)(2,1)S(1)}, u32[]{:S(2)}, u32[]{:S(2)}) async-start(bf16[4,512,128]{2,1,0:T(8,128)(2,1)} %bitcast.14), calls=%async_computation | async-start | bytes 1048576 | tf_op jit(solution)/shard_map/all_to_all | solution.py:396
  5.5 8.3 %all-to-all-done.frames = bf16[4,512,128]{2,1,0:T(8,128)(2,1)S(1)} async-done(((bf16[4,512,128]{2,1,0:T(8,128)(2,1)}), bf16[4,512,128]{2,1,0:T(8,128)(2,1)S(1)}, u32[]{:S(2)}, u32[]{:S(2)}) %all-to-all-start) | async-done | bytes 524320 | tf_op jit(solution)/shard_map/all_to_all | solution.py:396
  13.8 0.0 copy-start.1
  13.8 1.2 copy-done.1
  15.0 0.0 copy-start.2
  15.0 0.7 copy-done.2
  15.7 6.3 %gram.1 = (f32[2,128,1152]{2,1,0:T(8,128)S(1)}, f32[2,128,1152]{2,1,0:T(8,128)S(1)}) custom-call(s32[1]{0:T(128)} %bitcast.7.core.refs_0_, bf16[4,512,128]{2,1,0:T(8,128)(2,1)S(1)} %all-to-all-done.frames, bf16[512,1024]{1,0:T(8,128)(2,1)S(1)} %copy-done.1, f32[1,1024]{1,0:T(1,128)S(1)} %bitcast.13), custom_call_target="tpu_custom_call" | custom-call | flops 3500000000 | tf_op jit(solution)/shard_map/gram/pallas_call | solution.py:327
  22.0 2.2 %collective-permute-start.6 = (f32[2,128,1152]{2,1,0:T(8,128)S(1)}, f32[2,128,1152]{2,1,0:T(8,128)S(1)}, u32[]{:S(2)}, u32[]{:S(2)}) collective-permute-start(f32[2,128,1152]{2,1,0:T(8,128)S(1)} %get-tuple-element.21), channel_id=1, source_target_pairs={{0,4},{4,0},{1,5},{5,1},{2,6},{6,2},{3,7},{7,3},{8,12},{12,8},{9,1... | collective-permute-start | bytes 3538952 | tf_op jit(solution)/shard_map/ppermute | solution.py:416
  24.2 2.5 %collective-permute-done.6 = f32[2,128,1152]{2,1,0:T(8,128)S(1)} collective-permute-done((f32[2,128,1152]{2,1,0:T(8,128)S(1)}, f32[2,128,1152]{2,1,0:T(8,128)S(1)}, u32[]{:S(2)}, u32[]{:S(2)}) %collective-permute-start.6) | collective-permute-done | bytes 1179680 | tf_op jit(solution)/shard_map/ppermute | solution.py:416
  26.7 0.1 add.25
  26.9 0.3 reshape.26
  27.2 28.7 %all_to_all.25 = f32[64,4,1152]{2,1,0:T(4,128)S(1)} all-to-all(f32[64,4,1152]{2,1,0:T(4,128)S(1)} %reshape.26), channel_id=1, replica_groups=mesh['y'=4,'z'=4,'core'=2,'tgt'=4] {'y','z','tgt'}, dimensions={0} | all-to-all | bytes 2359296 | tf_op jit(solution)/shard_map/all_to_all | solution.py:396
  55.9 0.2 reduce_sum.18
  56.1 1.2 broadcast_in_dim.10
  57.3 4.8 %all-to-all-start.2 = ((f32[64,4,1152]{2,1,0:T(4,128)}), f32[64,4,1152]{2,1,0:T(4,128)S(1)}, u32[]{:S(2)}, u32[]{:S(2)}) async-start(f32[64,4,1152]{2,1,0:T(4,128)} %broadcast_in_dim.10), calls=%async_computation.2 | async-start | bytes 2359296 | tf_op jit(solution)/shard_map/all_to_all | solution.py:396
  62.1 0.0 copy-done.12
  62.1 0.0 copy-start.14
  62.1 0.0 copy-start.15
  62.2 2.2 %collective-permute-start.4 = (bf16[1024,128]{1,0:T(8,128)(2,1)S(1)}, bf16[1024,128]{1,0:T(8,128)(2,1)S(1)}, u32[]{:S(2)}, u32[]{:S(2)}) collective-permute-start(bf16[1024,128]{1,0:T(8,128)(2,1)S(1)} %get-tuple-element.30.refs_4_), channel_id=1, source_target_pairs={{0,3},{1,0},{2,1},{3,2},{4,7},{5,4},{6,5},{7,6},{8,11},{9,8},{10,9... | collective-permute-start | bytes 786440 | tf_op jit(solution)/shard_map/ppermute | solution.py:407
  64.3 0.0 collective-permute-start
  64.3 0.2 collective-permute-start.3
  64.6 2.5 %collective-permute-start.1 = (bf16[1024,128]{1,0:T(8,128)(2,1)S(1)}, bf16[1024,128]{1,0:T(8,128)(2,1)}, u32[]{:S(2)}, u32[]{:S(2)}) collective-permute-start(bf16[1024,128]{1,0:T(8,128)(2,1)S(1)} %get-tuple-element.31.refs_0_), channel_id=1, source_target_pairs={{0,3},{1,0},{2,1},{3,2},{4,7},{5,4},{6,5},{7,6},{8,11},{9,8},{10,9... | collective-permute-start | bytes 786440 | tf_op jit(solution)/shard_map/ppermute | solution.py:409
  67.0 13.1 %collective-permute-done.4.refs_6_ = bf16[1024,128]{1,0:T(8,128)(2,1)S(1)} collective-permute-done((bf16[1024,128]{1,0:T(8,128)(2,1)S(1)}, bf16[1024,128]{1,0:T(8,128)(2,1)S(1)}, u32[]{:S(2)}, u32[]{:S(2)}) %collective-permute-start.4) | collective-permute-done | bytes 262176 | tf_op jit(solution)/shard_map/ppermute | solution.py:407
  80.2 2.5 %collective-permute-start.5 = (bf16[1024,128]{1,0:T(8,128)(2,1)S(1)}, bf16[1024,128]{1,0:T(8,128)(2,1)}, u32[]{:S(2)}, u32[]{:S(2)}) collective-permute-start(bf16[1024,128]{1,0:T(8,128)(2,1)S(1)} %collective-permute-done.4.refs_6_), channel_id=1, source_target_pairs={{0,3},{1,0},{2,1},{3,2},{4,7},{5,4},{6,5},{7,6},{8,11},{9,8},{10,9... | collective-permute-start | bytes 786440 | tf_op jit(solution)/shard_map/ppermute | solution.py:411
  82.7 0.0 collective-permute-done.refs_1_
  82.7 0.0 collective-permute-start.2
  82.7 0.6 and_select_fusion.order
  83.3 0.0 all-to-all-done.2
  83.3 0.4 reshape.27.refs_1_
  83.7 0.0 copy-done.14
  83.7 0.0 copy-done.15
  83.7 0.0 copy-done.16
  83.7 0.0 copy-done.17
  83.8 0.0 copy-start.13
  83.8 4.5 %collective-permute-start.7 = (f32[2,128,1152]{2,1,0:T(8,128)S(1)}, f32[2,128,1152]{2,1,0:T(8,128)}, u32[]{:S(2)}, u32[]{:S(2)}) collective-permute-start(f32[2,128,1152]{2,1,0:T(8,128)S(1)} %reshape.27.refs_1_), channel_id=1, source_target_pairs={{0,4},{4,0},{1,5},{5,1},{2,6},{6,2},{3,7},{7,3},{8,12},{12,8},{9,1... | collective-permute-start | bytes 3538952 | tf_op jit(solution)/shard_map/ppermute | solution.py:423
  88.2 0.0 collective-permute-done.3.refs_5_
  88.2 0.0 collective-permute-done.1.refs_2_
  88.2 3.3 %collective-permute-done.5.refs_7_ = bf16[1024,128]{1,0:T(8,128)(2,1)} collective-permute-done((bf16[1024,128]{1,0:T(8,128)(2,1)S(1)}, bf16[1024,128]{1,0:T(8,128)(2,1)}, u32[]{:S(2)}, u32[]{:S(2)}) %collective-permute-start.5) | collective-permute-done | bytes 262176 | tf_op jit(solution)/shard_map/ppermute | solution.py:411
  91.5 2.2 %collective-permute-done.2.refs_3_ = bf16[1024,128]{1,0:T(8,128)(2,1)} collective-permute-done((bf16[1024,128]{1,0:T(8,128)(2,1)S(1)}, bf16[1024,128]{1,0:T(8,128)(2,1)}, u32[]{:S(2)}, u32[]{:S(2)}) %collective-permute-start.2) | collective-permute-done | bytes 262176 | tf_op jit(solution)/shard_map/ppermute | solution.py:410
  93.7 16.5 %features.1 = (bf16[2048,1024]{1,0:T(8,128)(2,1)}, bf16[2048,1024]{1,0:T(8,128)(2,1)}, f32[1024,256]{1,0:T(8,128)}) custom-call(s32[4]{0:T(128)} %and_select_fusion.order, bf16[1024,128]{1,0:T(8,128)(2,1)} %copy-done.15, bf16[1024,128]{1,0:T(8,128)(2,1)} %copy-done.17, bf16[1024,128]{1,0:T(8,128)(2,1)} %collective-permute-done.1.refs_2_, ...), custom_call_target="tpu_custom_call" | custom-call | flops 7500000256 | tf_op jit(solution)/shard_map/features/pallas_call | solution.py:343
  110.2 0.0 copy-done.13
  110.2 21.6 %all_to_all.26 = f32[16,64,256]{2,1,0:T(8,128)S(1)} all-to-all(f32[16,64,256]{2,1,0:T(8,128)} %bitcast.15), channel_id=1, replica_groups=mesh['y'=4,'z'=4,'core'=2,'tgt'=4] {'y','z'}, dimensions={0} | all-to-all | bytes 2097152 | tf_op jit(solution)/shard_map/all_to_all | solution.py:396
  131.8 0.1 reduce_sum.19
  131.9 3.2 %collective-permute-start.8 = (f32[64,256]{1,0:T(8,128)S(1)}, f32[64,256]{1,0:T(8,128)S(1)}, u32[]{:S(2)}, u32[]{:S(2)}) collective-permute-start(f32[64,256]{1,0:T(8,128)S(1)} %reduce_sum.19), channel_id=1, source_target_pairs={{0,4},{4,0},{1,5},{5,1},{2,6},{6,2},{3,7},{7,3},{8,12},{12,8},{9,1... | collective-permute-start | bytes 196616 | tf_op jit(solution)/shard_map/ppermute | solution.py:431
  135.1 0.9 collective-permute-done.8
  136.0 1.1 broadcast_in_dim.22
  137.1 3.7 %all-to-all-start.4 = ((f32[16,64,256]{2,1,0:T(8,128)}), f32[16,64,256]{2,1,0:T(8,128)S(1)}, u32[]{:S(2)}, u32[]{:S(2)}) async-start(f32[16,64,256]{2,1,0:T(8,128)} %broadcast_in_dim.22), calls=%async_computation.4 | async-start | bytes 2097152 | tf_op jit(solution)/shard_map/all_to_all | solution.py:396
  140.8 0.0 collective-permute-done.7.refs_2_
  140.8 21.3 %factor0.1 = (bf16[4,128,1024]{2,1,0:T(8,128)(2,1)}, bf16[4,128,1024]{2,1,0:T(8,128)(2,1)}, f32[4,128,128]{2,1,0:T(8,128)}, f32[4,128,512]{2,1,0:T(8,128)}) custom-call(s32[1]{0:T(128)} %bitcast.7.core.refs_0_, f32[2,128,1152]{2,1,0:T(8,128)} %copy-done.13, f32[2,128,1152]{2,1,0:T(8,128)} %collective-permute-done.7.refs_2_), custom_call_target="tpu_custom_call" | custom-call | flops 14000000000 | tf_op jit(solution)/shard_map/factor0/pallas_call | solution.py:282
  162.1 18.4 %factor1.1 = (bf16[4,128,512]{2,1,0:T(8,128)(2,1)}, bf16[4,128,512]{2,1,0:T(8,128)(2,1)}, f32[4,128,128]{2,1,0:T(8,128)}) custom-call(f32[4,128,512]{2,1,0:T(8,128)} %get-tuple-element.25.refs_0_), custom_call_target="tpu_custom_call" | custom-call | flops 11000000512 | tf_op jit(solution)/shard_map/factor1/pallas_call | solution.py:301
  180.5 0.0 all-to-all-done.4
  180.5 0.0 copy-done.6
  180.5 0.0 copy-done.7
  180.5 0.0 copy-done.10
  180.5 0.0 copy-start.8
  180.5 1.0 copy-done.8
  181.6 1.0 copy-done.9
  182.6 0.9 copy-done.11
  183.6 5.5 %solve.1.coef = f32[1024,256]{1,0:T(8,128)} custom-call(bf16[4,128,1024]{2,1,0:T(8,128)(2,1)S(1)} %copy-done.6, bf16[4,128,1024]{2,1,0:T(8,128)(2,1)S(1)} %copy-done.7, f32[4,128,128]{2,1,0:T(8,128)S(1)} %copy-done.10, bf16[4,128,512]{2,1,0:T(8,128)(2,1)S(1)} %copy-done.8, bf16[4,128,512]{2,1,0:T(8,128)(2,1)S(1)} %copy-done.9, ...), custom_call_target="tpu_custom_call" | custom-call | flops 6000000000 | tf_op jit(solution)/shard_map/solve/pallas_call | solution.py:312
  189.1 0.0 copy-done
  189.1 0.0 copy-done.4
  189.1 0.0 copy-done.5
  189.1 1.2 copy-done.3
  190.3 5.7 %update.1 = f32[2048,256]{1,0:T(8,128)} custom-call(bf16[2048,1024]{1,0:T(8,128)(2,1)S(1)} %copy-done.4, bf16[2048,1024]{1,0:T(8,128)(2,1)S(1)} %copy-done.5, f32[1024,256]{1,0:T(8,128)S(1)} %copy-done.3, f32[2048,256]{1,0:T(8,128)S(1)} %copy-done), custom_call_target="tpu_custom_call" | custom-call | flops 5000000000 | tf_op jit(solution)/shard_map/update/pallas_call | solution.py:373
  (14 shorter events, 0.1 us)
Async XLA Ops:
  0.6 13.2 %all-to-all-start = ((bf16[4,512,128]{2,1,0:T(8,128)(2,1)}), bf16[4,512,128]{2,1,0:T(8,128)(2,1)S(1)}, u32[]{:S(2)}, u32[]{:S(2)}) async-start(bf16[4,512,128]{2,1,0:T(8,128)(2,1)} %bitcast.14), calls=%async_computation | async-start | bytes 1048576 | tf_op jit(solution)/shard_map/all_to_all | solution.py:396
  13.8 1.2 copy-start.1
  15.0 0.7 copy-start.2
  22.0 4.7 %collective-permute-start.6 = (f32[2,128,1152]{2,1,0:T(8,128)S(1)}, f32[2,128,1152]{2,1,0:T(8,128)S(1)}, u32[]{:S(2)}, u32[]{:S(2)}) collective-permute-start(f32[2,128,1152]{2,1,0:T(8,128)S(1)} %get-tuple-element.21), channel_id=1, source_target_pairs={{0,4},{4,0},{1,5},{5,1},{2,6},{6,2},{3,7},{7,3},{8,12},{12,8},{9,1... | collective-permute-start | bytes 3538952 | tf_op jit(solution)/shard_map/ppermute | solution.py:416
  57.3 4.8 %copy-start.12 = (bf16[2048,128]{1,0:T(8,128)(2,1)S(1)}, bf16[2048,128]{1,0:T(8,128)(2,1)}, u32[]{:S(2)}) copy-start(bf16[2048,128]{1,0:T(8,128)(2,1)} %param.4) | copy-start | bytes 1572868
  57.3 26.0 %all-to-all-start.2 = ((f32[64,4,1152]{2,1,0:T(4,128)}), f32[64,4,1152]{2,1,0:T(4,128)S(1)}, u32[]{:S(2)}, u32[]{:S(2)}) async-start(f32[64,4,1152]{2,1,0:T(4,128)} %broadcast_in_dim.10), calls=%async_computation.2 | async-start | bytes 2359296 | tf_op jit(solution)/shard_map/all_to_all | solution.py:396
  62.1 21.6 %copy-start.14 = (bf16[1024,128]{1,0:T(8,128)(2,1)}, bf16[1024,128]{1,0:T(8,128)(2,1)S(1)}, u32[]{:S(2)}) copy-start(bf16[1024,128]{1,0:T(8,128)(2,1)S(1)} %get-tuple-element.30.refs_4_) | copy-start | bytes 786436
  62.1 21.6 %copy-start.15 = (bf16[1024,128]{1,0:T(8,128)(2,1)}, bf16[1024,128]{1,0:T(8,128)(2,1)S(1)}, u32[]{:S(2)}) copy-start(bf16[1024,128]{1,0:T(8,128)(2,1)S(1)} %get-tuple-element.31.refs_0_) | copy-start | bytes 786436
  62.2 18.0 %collective-permute-start.4 = (bf16[1024,128]{1,0:T(8,128)(2,1)S(1)}, bf16[1024,128]{1,0:T(8,128)(2,1)S(1)}, u32[]{:S(2)}, u32[]{:S(2)}) collective-permute-start(bf16[1024,128]{1,0:T(8,128)(2,1)S(1)} %get-tuple-element.30.refs_4_), channel_id=1, source_target_pairs={{0,3},{1,0},{2,1},{3,2},{4,7},{5,4},{6,5},{7,6},{8,11},{9,8},{10,9... | collective-permute-start | bytes 786440 | tf_op jit(solution)/shard_map/ppermute | solution.py:407
  64.3 18.3 %collective-permute-start = (bf16[1024,128]{1,0:T(8,128)(2,1)S(1)}, bf16[1024,128]{1,0:T(8,128)(2,1)S(1)}, u32[]{:S(2)}, u32[]{:S(2)}) collective-permute-start(bf16[1024,128]{1,0:T(8,128)(2,1)S(1)} %get-tuple-element.31.refs_0_), channel_id=1, source_target_pairs={{0,1},{1,2},{2,3},{3,0},{4,5},{5,6},{6,7},{7,4},{8,9},{9,10},{10,1... | collective-permute-start | bytes 786440 | tf_op jit(solution)/shard_map/ppermute | solution.py:406
  64.3 23.9 %collective-permute-start.3 = (bf16[1024,128]{1,0:T(8,128)(2,1)S(1)}, bf16[1024,128]{1,0:T(8,128)(2,1)}, u32[]{:S(2)}, u32[]{:S(2)}) collective-permute-start(bf16[1024,128]{1,0:T(8,128)(2,1)S(1)} %get-tuple-element.30.refs_4_), channel_id=1, source_target_pairs={{0,1},{1,2},{2,3},{3,0},{4,5},{5,6},{6,7},{7,4},{8,9},{9,10},{10,1... | collective-permute-start | bytes 786440 | tf_op jit(solution)/shard_map/ppermute | solution.py:408
  64.6 23.6 %collective-permute-start.1 = (bf16[1024,128]{1,0:T(8,128)(2,1)S(1)}, bf16[1024,128]{1,0:T(8,128)(2,1)}, u32[]{:S(2)}, u32[]{:S(2)}) collective-permute-start(bf16[1024,128]{1,0:T(8,128)(2,1)S(1)} %get-tuple-element.31.refs_0_), channel_id=1, source_target_pairs={{0,3},{1,0},{2,1},{3,2},{4,7},{5,4},{6,5},{7,6},{8,11},{9,8},{10,9... | collective-permute-start | bytes 786440 | tf_op jit(solution)/shard_map/ppermute | solution.py:409
  80.2 3.6 %copy-start.16 = (bf16[1024,128]{1,0:T(8,128)(2,1)}, bf16[1024,128]{1,0:T(8,128)(2,1)S(1)}, u32[]{:S(2)}) copy-start(bf16[1024,128]{1,0:T(8,128)(2,1)S(1)} %collective-permute-done.4.refs_6_) | copy-start | bytes 786436
  80.2 11.3 %collective-permute-start.5 = (bf16[1024,128]{1,0:T(8,128)(2,1)S(1)}, bf16[1024,128]{1,0:T(8,128)(2,1)}, u32[]{:S(2)}, u32[]{:S(2)}) collective-permute-start(bf16[1024,128]{1,0:T(8,128)(2,1)S(1)} %collective-permute-done.4.refs_6_), channel_id=1, source_target_pairs={{0,3},{1,0},{2,1},{3,2},{4,7},{5,4},{6,5},{7,6},{8,11},{9,8},{10,9... | collective-permute-start | bytes 786440 | tf_op jit(solution)/shard_map/ppermute | solution.py:411
  82.7 1.1 copy-start.17
  82.7 11.0 %collective-permute-start.2 = (bf16[1024,128]{1,0:T(8,128)(2,1)S(1)}, bf16[1024,128]{1,0:T(8,128)(2,1)}, u32[]{:S(2)}, u32[]{:S(2)}) collective-permute-start(bf16[1024,128]{1,0:T(8,128)(2,1)S(1)} %collective-permute-done.refs_1_), channel_id=1, source_target_pairs={{0,1},{1,2},{2,3},{3,0},{4,5},{5,6},{6,7},{7,4},{8,9},{9,10},{10,1... | collective-permute-start | bytes 786440 | tf_op jit(solution)/shard_map/ppermute | solution.py:410
  83.8 26.4 %copy-start.13 = (f32[2,128,1152]{2,1,0:T(8,128)}, f32[2,128,1152]{2,1,0:T(8,128)S(1)}, u32[]{:S(2)}) copy-start(f32[2,128,1152]{2,1,0:T(8,128)S(1)} %reshape.27.refs_1_) | copy-start | bytes 3538948
  83.8 57.0 %collective-permute-start.7 = (f32[2,128,1152]{2,1,0:T(8,128)S(1)}, f32[2,128,1152]{2,1,0:T(8,128)}, u32[]{:S(2)}, u32[]{:S(2)}) collective-permute-start(f32[2,128,1152]{2,1,0:T(8,128)S(1)} %reshape.27.refs_1_), channel_id=1, source_target_pairs={{0,4},{4,0},{1,5},{5,1},{2,6},{6,2},{3,7},{7,3},{8,12},{12,8},{9,1... | collective-permute-start | bytes 3538952 | tf_op jit(solution)/shard_map/ppermute | solution.py:423
  131.9 4.1 %collective-permute-start.8 = (f32[64,256]{1,0:T(8,128)S(1)}, f32[64,256]{1,0:T(8,128)S(1)}, u32[]{:S(2)}, u32[]{:S(2)}) collective-permute-start(f32[64,256]{1,0:T(8,128)S(1)} %reduce_sum.19), channel_id=1, source_target_pairs={{0,4},{4,0},{1,5},{5,1},{2,6},{6,2},{3,7},{7,3},{8,12},{12,8},{9,1... | collective-permute-start | bytes 196616 | tf_op jit(solution)/shard_map/ppermute | solution.py:431
  137.1 43.4 %all-to-all-start.4 = ((f32[16,64,256]{2,1,0:T(8,128)}), f32[16,64,256]{2,1,0:T(8,128)S(1)}, u32[]{:S(2)}, u32[]{:S(2)}) async-start(f32[16,64,256]{2,1,0:T(8,128)} %broadcast_in_dim.22), calls=%async_computation.4 | async-start | bytes 2097152 | tf_op jit(solution)/shard_map/all_to_all | solution.py:396
  162.1 18.4 %copy-start.6 = (bf16[4,128,1024]{2,1,0:T(8,128)(2,1)S(1)}, bf16[4,128,1024]{2,1,0:T(8,128)(2,1)}, u32[]{:S(2)}) copy-start(bf16[4,128,1024]{2,1,0:T(8,128)(2,1)} %get-tuple-element.22.high0) | copy-start | bytes 3145732
  162.1 18.4 %copy-start.7 = (bf16[4,128,1024]{2,1,0:T(8,128)(2,1)S(1)}, bf16[4,128,1024]{2,1,0:T(8,128)(2,1)}, u32[]{:S(2)}) copy-start(bf16[4,128,1024]{2,1,0:T(8,128)(2,1)} %get-tuple-element.23.low0) | copy-start | bytes 3145732
  162.1 18.4 %copy-start.10 = (f32[4,128,128]{2,1,0:T(8,128)S(1)}, f32[4,128,128]{2,1,0:T(8,128)}, u32[]{:S(2)}) copy-start(f32[4,128,128]{2,1,0:T(8,128)} %get-tuple-element.24.inverse0) | copy-start | bytes 786436
  180.5 1.0 copy-start.8
  181.6 1.0 copy-start.9
  182.6 0.9 copy-start.11
  183.6 5.5 %copy-start = (f32[2048,256]{1,0:T(8,128)S(1)}, f32[2048,256]{1,0:T(8,128)}, u32[]{:S(2)}) copy-start(f32[2048,256]{1,0:T(8,128)} %residual.1) | copy-start | bytes 6291460
  183.6 5.5 %copy-start.4 = (bf16[2048,1024]{1,0:T(8,128)(2,1)S(1)}, bf16[2048,1024]{1,0:T(8,128)(2,1)}, u32[]{:S(2)}) copy-start(bf16[2048,1024]{1,0:T(8,128)(2,1)} %get-tuple-element.17.high) | copy-start | bytes 12582916
  183.6 5.5 %copy-start.5 = (bf16[2048,1024]{1,0:T(8,128)(2,1)S(1)}, bf16[2048,1024]{1,0:T(8,128)(2,1)}, u32[]{:S(2)}) copy-start(bf16[2048,1024]{1,0:T(8,128)(2,1)} %get-tuple-element.18.low) | copy-start | bytes 12582916
  189.1 1.2 copy-start.3

commit v2 on v1

--- a/solution.py
+++ b/solution.py
@@ -335,7 +335,7 @@
     )(core, frames, weights, phases)
 
 
-def feature_call(order, tops, bottoms, weights, phases, residual, tile=256):
+def feature_call(order, tops, bottoms, weights, phases, residual, tile=512):
     rows, cols = residual.shape
     width = tops[0].shape[1]
     feat = weights.shape[1]
@@ -413,7 +413,8 @@
 
 
 def summed_gram(mine, other):
-    mine = mine + lax.ppermute(other, "core", SWAP)
+    other = lax.ppermute(other, "core", SWAP)
+    mine = mine + other
     chips = ("y", "z", "tgt")
     count = lax.axis_size(chips)
     parts = mine.reshape(count, -1, mine.shape[-1])
@@ -440,11 +441,10 @@
     core = lax.axis_index("core")
     at = lax.axis_index("tgt")
     whole_rows = exchange(frames.reshape(4, rows_here // 4, -1), "tgt")
-    whole_rows, own = lax.optimization_barrier((whole_rows, frames))
-    tops, bottoms = ring_slabs(own)
+    order = jnp.stack([at, at + 3, at + 1, at + 2]) % 4
+    tops, bottoms = ring_slabs(frames)
     halves = gram_call(core[None], whole_rows, weights, phases)
     mine, other = summed_gram(*halves)
-    order = jnp.stack([at, at + 3, at + 1, at + 2]) % 4
     high, low, corr = feature_call(order, tops, bottoms, weights, phases, residual)
     corr = summed_corr(corr)
     *factor0, rest = first_factor_call(core[None], mine, other, ridge)

time: 197 us -> 195 us (0.990)
  transfers between devices with their start and end apart: 12 -> 12, of which waited for: 6 -> 6; matrix products, arithmetic and copies ran while one was open for 1% -> 1% of each run, Pallas kernels for 29% -> 28%
where the time goes in v2:
time: 195 us
  Pallas kernels  72.2 us (37%)
  blocking collectives  50.3 us (26%)
  starting transfers between devices  30.6 us (16%)
  waiting for transfers between devices  30.3 us (16%)
  local copies, waits for them, and re-layouts  9.25 us (5%)
    all_to_all x2, blocking collectives, exchange(): return lax.all_to_all(parts, axes, 0, 0, tiled=True)  50.3 us
    pallas_call x1, Pallas kernels, first_factor_call(): pl.pallas_call(lambda *refs: first_factor_kernel(*refs, ridge=ridge), in_...  21.3 us
    pallas_call x1, Pallas kernels, second_factor_call(): pl.pallas_call(lambda *refs: second_factor_kernel(*refs, ridge=ridge), ou...  18.4 us
    pallas_call x1, Pallas kernels, feature_call(): pl.pallas_call(feature_kernel, grid=(rows // tile,), in_specs=[pl.BlockSp...  15 us
    all_to_all x3, starting transfers between devices, exchange(): return lax.all_to_all(parts, axes, 0, 0, tiled=True)  13.3 us
    ppermute x1, waiting for transfers between devices, ring_slabs(): right_bottom = lax.ppermute(bottom, 'tgt', DOWN)  13.1 us
    all_to_all x3, waiting for transfers between devices, exchange(): return lax.all_to_all(parts, axes, 0, 0, tiled=True)  8.33 us
    pallas_call x1, Pallas kernels, gram_call(): pl.pallas_call(gram_kernel, in_specs=[pl.BlockSpec(memory_space=pltpu.SME...  6.32 us
  transfers between devices with their start and end apart: 12, of which 6 were waited for; matrix products, arithmetic and copies ran while one was open for 1% of the time, Pallas kernels for 28%

profile of v2, /device:TPU:1, one launch (start us, length us, event | category | flops | bytes accessed | tf_op | source)
XLA Modules:
  0.0 194.5 jit_solution(2745986484187110747)
XLA Ops:
  0.6 4.8 %all-to-all-start = ((bf16[4,512,128]{2,1,0:T(8,128)(2,1)}), bf16[4,512,128]{2,1,0:T(8,128)(2,1)S(1)}, u32[]{:S(2)}, u32[]{:S(2)}) async-start(bf16[4,512,128]{2,1,0:T(8,128)(2,1)} %bitcast.14), calls=%async_computation | async-start | bytes 1048576 | tf_op jit(solution)/shard_map/all_to_all | solution.py:396
  5.5 8.3 %all-to-all-done.frames = bf16[4,512,128]{2,1,0:T(8,128)(2,1)S(1)} async-done(((bf16[4,512,128]{2,1,0:T(8,128)(2,1)}), bf16[4,512,128]{2,1,0:T(8,128)(2,1)S(1)}, u32[]{:S(2)}, u32[]{:S(2)}) %all-to-all-start) | async-done | bytes 524320 | tf_op jit(solution)/shard_map/all_to_all | solution.py:396
  13.8 0.0 copy-start.1
  13.8 1.2 copy-done.1
  15.0 0.0 copy-start.2
  15.0 0.7 copy-done.2
  15.7 6.3 %gram.1 = (f32[2,128,1152]{2,1,0:T(8,128)S(1)}, f32[2,128,1152]{2,1,0:T(8,128)S(1)}) custom-call(s32[1]{0:T(128)} %bitcast.6.core.refs_0_, bf16[4,512,128]{2,1,0:T(8,128)(2,1)S(1)} %all-to-all-done.frames, bf16[512,1024]{1,0:T(8,128)(2,1)S(1)} %copy-done.1, f32[1,1024]{1,0:T(1,128)S(1)} %bitcast.13), custom_call_target="tpu_custom_call" | custom-call | flops 3500000000 | tf_op jit(solution)/shard_map/gram/pallas_call | solution.py:327
  22.0 2.2 %collective-permute-start.6 = (f32[2,128,1152]{2,1,0:T(8,128)S(1)}, f32[2,128,1152]{2,1,0:T(8,128)S(1)}, u32[]{:S(2)}, u32[]{:S(2)}) collective-permute-start(f32[2,128,1152]{2,1,0:T(8,128)S(1)} %get-tuple-element.17), channel_id=1, source_target_pairs={{0,4},{4,0},{1,5},{5,1},{2,6},{6,2},{3,7},{7,3},{8,12},{12,8},{9,1... | collective-permute-start | bytes 3538952 | tf_op jit(solution)/shard_map/ppermute | solution.py:416
  24.2 2.5 %collective-permute-done.6 = f32[2,128,1152]{2,1,0:T(8,128)S(1)} collective-permute-done((f32[2,128,1152]{2,1,0:T(8,128)S(1)}, f32[2,128,1152]{2,1,0:T(8,128)S(1)}, u32[]{:S(2)}, u32[]{:S(2)}) %collective-permute-start.6) | collective-permute-done | bytes 1179680 | tf_op jit(solution)/shard_map/ppermute | solution.py:416
  26.7 0.1 add.25
  26.9 0.3 reshape.26
  27.2 28.7 %all_to_all.25 = f32[64,4,1152]{2,1,0:T(4,128)S(1)} all-to-all(f32[64,4,1152]{2,1,0:T(4,128)S(1)} %reshape.26), channel_id=1, replica_groups=mesh['y'=4,'z'=4,'core'=2,'tgt'=4] {'y','z','tgt'}, dimensions={0} | all-to-all | bytes 2359296 | tf_op jit(solution)/shard_map/all_to_all | solution.py:396
  55.9 0.2 reduce_sum.18
  56.1 1.2 broadcast_in_dim.10
  57.3 4.8 %all-to-all-start.2 = ((f32[64,4,1152]{2,1,0:T(4,128)}), f32[64,4,1152]{2,1,0:T(4,128)S(1)}, u32[]{:S(2)}, u32[]{:S(2)}) async-start(f32[64,4,1152]{2,1,0:T(4,128)} %broadcast_in_dim.10), calls=%async_computation.2 | async-start | bytes 2359296 | tf_op jit(solution)/shard_map/all_to_all | solution.py:396
  62.1 0.0 copy-done.12
  62.1 0.0 copy-start.14
  62.1 0.0 copy-start.15
  62.2 2.2 %collective-permute-start.4 = (bf16[1024,128]{1,0:T(8,128)(2,1)S(1)}, bf16[1024,128]{1,0:T(8,128)(2,1)S(1)}, u32[]{:S(2)}, u32[]{:S(2)}) collective-permute-start(bf16[1024,128]{1,0:T(8,128)(2,1)S(1)} %get-tuple-element.26.refs_4_), channel_id=1, source_target_pairs={{0,3},{1,0},{2,1},{3,2},{4,7},{5,4},{6,5},{7,6},{8,11},{9,8},{10,9... | collective-permute-start | bytes 786440 | tf_op jit(solution)/shard_map/ppermute | solution.py:407
  64.3 0.0 collective-permute-start
  64.3 0.2 collective-permute-start.3
  64.6 2.5 %collective-permute-start.1 = (bf16[1024,128]{1,0:T(8,128)(2,1)S(1)}, bf16[1024,128]{1,0:T(8,128)(2,1)}, u32[]{:S(2)}, u32[]{:S(2)}) collective-permute-start(bf16[1024,128]{1,0:T(8,128)(2,1)S(1)} %get-tuple-element.27.refs_0_), channel_id=1, source_target_pairs={{0,3},{1,0},{2,1},{3,2},{4,7},{5,4},{6,5},{7,6},{8,11},{9,8},{10,9... | collective-permute-start | bytes 786440 | tf_op jit(solution)/shard_map/ppermute | solution.py:409
  67.0 13.1 %collective-permute-done.4.refs_6_ = bf16[1024,128]{1,0:T(8,128)(2,1)S(1)} collective-permute-done((bf16[1024,128]{1,0:T(8,128)(2,1)S(1)}, bf16[1024,128]{1,0:T(8,128)(2,1)S(1)}, u32[]{:S(2)}, u32[]{:S(2)}) %collective-permute-start.4) | collective-permute-done | bytes 262176 | tf_op jit(solution)/shard_map/ppermute | solution.py:407
  80.2 2.5 %collective-permute-start.5 = (bf16[1024,128]{1,0:T(8,128)(2,1)S(1)}, bf16[1024,128]{1,0:T(8,128)(2,1)}, u32[]{:S(2)}, u32[]{:S(2)}) collective-permute-start(bf16[1024,128]{1,0:T(8,128)(2,1)S(1)} %collective-permute-done.4.refs_6_), channel_id=1, source_target_pairs={{0,3},{1,0},{2,1},{3,2},{4,7},{5,4},{6,5},{7,6},{8,11},{9,8},{10,9... | collective-permute-start | bytes 786440 | tf_op jit(solution)/shard_map/ppermute | solution.py:411
  82.7 0.0 collective-permute-done.refs_1_
  82.7 0.0 collective-permute-start.2
  82.7 0.6 and_select_fusion.order
  83.3 0.0 all-to-all-done.2
  83.3 0.4 reshape.27.refs_1_
  83.7 0.0 copy-done.14
  83.7 0.0 copy-done.15
  83.7 0.0 copy-done.16
  83.7 0.0 copy-done.17
  83.8 0.0 copy-start.13
  83.8 4.5 %collective-permute-start.7 = (f32[2,128,1152]{2,1,0:T(8,128)S(1)}, f32[2,128,1152]{2,1,0:T(8,128)}, u32[]{:S(2)}, u32[]{:S(2)}) collective-permute-start(f32[2,128,1152]{2,1,0:T(8,128)S(1)} %reshape.27.refs_1_), channel_id=1, source_target_pairs={{0,4},{4,0},{1,5},{5,1},{2,6},{6,2},{3,7},{7,3},{8,12},{12,8},{9,1... | collective-permute-start | bytes 3538952 | tf_op jit(solution)/shard_map/ppermute | solution.py:424
  88.2 0.0 collective-permute-done.3.refs_5_
  88.2 0.0 collective-permute-done.1.refs_2_
  88.2 3.3 %collective-permute-done.5.refs_7_ = bf16[1024,128]{1,0:T(8,128)(2,1)} collective-permute-done((bf16[1024,128]{1,0:T(8,128)(2,1)S(1)}, bf16[1024,128]{1,0:T(8,128)(2,1)}, u32[]{:S(2)}, u32[]{:S(2)}) %collective-permute-start.5) | collective-permute-done | bytes 262176 | tf_op jit(solution)/shard_map/ppermute | solution.py:411
  91.5 2.2 %collective-permute-done.2.refs_3_ = bf16[1024,128]{1,0:T(8,128)(2,1)} collective-permute-done((bf16[1024,128]{1,0:T(8,128)(2,1)S(1)}, bf16[1024,128]{1,0:T(8,128)(2,1)}, u32[]{:S(2)}, u32[]{:S(2)}) %collective-permute-start.2) | collective-permute-done | bytes 262176 | tf_op jit(solution)/shard_map/ppermute | solution.py:410
  93.7 15.0 %features.1 = (bf16[2048,1024]{1,0:T(8,128)(2,1)}, bf16[2048,1024]{1,0:T(8,128)(2,1)}, f32[1024,256]{1,0:T(8,128)}) custom-call(s32[4]{0:T(128)} %and_select_fusion.order, bf16[1024,128]{1,0:T(8,128)(2,1)} %copy-done.15, bf16[1024,128]{1,0:T(8,128)(2,1)} %copy-done.17, bf16[1024,128]{1,0:T(8,128)(2,1)} %collective-permute-done.1.refs_2_, ...), custom_call_target="tpu_custom_call" | custom-call | flops 7500000256 | tf_op jit(solution)/shard_map/features/pallas_call | solution.py:343
  108.7 0.0 copy-done.13
  108.7 21.6 %all_to_all.26 = f32[16,64,256]{2,1,0:T(8,128)S(1)} all-to-all(f32[16,64,256]{2,1,0:T(8,128)} %bitcast.15), channel_id=1, replica_groups=mesh['y'=4,'z'=4,'core'=2,'tgt'=4] {'y','z'}, dimensions={0} | all-to-all | bytes 2097152 | tf_op jit(solution)/shard_map/all_to_all | solution.py:396
  130.4 0.1 reduce_sum.19
  130.4 3.2 %collective-permute-start.8 = (f32[64,256]{1,0:T(8,128)S(1)}, f32[64,256]{1,0:T(8,128)S(1)}, u32[]{:S(2)}, u32[]{:S(2)}) collective-permute-start(f32[64,256]{1,0:T(8,128)S(1)} %reduce_sum.19), channel_id=1, source_target_pairs={{0,4},{4,0},{1,5},{5,1},{2,6},{6,2},{3,7},{7,3},{8,12},{12,8},{9,1... | collective-permute-start | bytes 196616 | tf_op jit(solution)/shard_map/ppermute | solution.py:432
  133.6 0.9 collective-permute-done.8
  134.6 1.1 broadcast_in_dim.22
  135.6 3.7 %all-to-all-start.4 = ((f32[16,64,256]{2,1,0:T(8,128)}), f32[16,64,256]{2,1,0:T(8,128)S(1)}, u32[]{:S(2)}, u32[]{:S(2)}) async-start(f32[16,64,256]{2,1,0:T(8,128)} %broadcast_in_dim.22), calls=%async_computation.4 | async-start | bytes 2097152 | tf_op jit(solution)/shard_map/all_to_all | solution.py:396
  139.3 0.0 collective-permute-done.7.refs_2_
  139.3 21.3 %factor0.1 = (bf16[4,128,1024]{2,1,0:T(8,128)(2,1)}, bf16[4,128,1024]{2,1,0:T(8,128)(2,1)}, f32[4,128,128]{2,1,0:T(8,128)}, f32[4,128,512]{2,1,0:T(8,128)}) custom-call(s32[1]{0:T(128)} %bitcast.6.core.refs_0_, f32[2,128,1152]{2,1,0:T(8,128)} %copy-done.13, f32[2,128,1152]{2,1,0:T(8,128)} %collective-permute-done.7.refs_2_), custom_call_target="tpu_custom_call" | custom-call | flops 14000000000 | tf_op jit(solution)/shard_map/factor0/pallas_call | solution.py:282
  160.6 18.4 %factor1.1 = (bf16[4,128,512]{2,1,0:T(8,128)(2,1)}, bf16[4,128,512]{2,1,0:T(8,128)(2,1)}, f32[4,128,128]{2,1,0:T(8,128)}) custom-call(f32[4,128,512]{2,1,0:T(8,128)} %get-tuple-element.21.refs_0_), custom_call_target="tpu_custom_call" | custom-call | flops 11000000512 | tf_op jit(solution)/shard_map/factor1/pallas_call | solution.py:301
  179.0 0.0 all-to-all-done.4
  179.0 0.0 copy-done.6
  179.0 0.0 copy-done.7
  179.0 0.0 copy-done.10
  179.0 0.0 copy-start.8
  179.0 1.0 copy-done.8
  180.1 1.0 copy-done.9
  181.1 0.9 copy-done.11
  182.1 5.5 %solve.1.coef = f32[1024,256]{1,0:T(8,128)} custom-call(bf16[4,128,1024]{2,1,0:T(8,128)(2,1)S(1)} %copy-done.6, bf16[4,128,1024]{2,1,0:T(8,128)(2,1)S(1)} %copy-done.7, f32[4,128,128]{2,1,0:T(8,128)S(1)} %copy-done.10, bf16[4,128,512]{2,1,0:T(8,128)(2,1)S(1)} %copy-done.8, bf16[4,128,512]{2,1,0:T(8,128)(2,1)S(1)} %copy-done.9, ...), custom_call_target="tpu_custom_call" | custom-call | flops 6000000000 | tf_op jit(solution)/shard_map/solve/pallas_call | solution.py:312
  187.6 0.0 copy-done
  187.6 0.0 copy-done.4
  187.6 0.0 copy-done.5
  187.6 1.2 copy-done.3
  188.8 5.7 %update.1 = f32[2048,256]{1,0:T(8,128)} custom-call(bf16[2048,1024]{1,0:T(8,128)(2,1)S(1)} %copy-done.4, bf16[2048,1024]{1,0:T(8,128)(2,1)S(1)} %copy-done.5, f32[1024,256]{1,0:T(8,128)S(1)} %copy-done.3, f32[2048,256]{1,0:T(8,128)S(1)} %copy-done), custom_call_target="tpu_custom_call" | custom-call | flops 5000000000 | tf_op jit(solution)/shard_map/update/pallas_call | solution.py:373
  (14 shorter events, 0.1 us)
Async XLA Ops:
  0.6 13.2 %all-to-all-start = ((bf16[4,512,128]{2,1,0:T(8,128)(2,1)}), bf16[4,512,128]{2,1,0:T(8,128)(2,1)S(1)}, u32[]{:S(2)}, u32[]{:S(2)}) async-start(bf16[4,512,128]{2,1,0:T(8,128)(2,1)} %bitcast.14), calls=%async_computation | async-start | bytes 1048576 | tf_op jit(solution)/shard_map/all_to_all | solution.py:396
  13.8 1.2 copy-start.1
  15.0 0.7 copy-start.2
  22.0 4.7 %collective-permute-start.6 = (f32[2,128,1152]{2,1,0:T(8,128)S(1)}, f32[2,128,1152]{2,1,0:T(8,128)S(1)}, u32[]{:S(2)}, u32[]{:S(2)}) collective-permute-start(f32[2,128,1152]{2,1,0:T(8,128)S(1)} %get-tuple-element.17), channel_id=1, source_target_pairs={{0,4},{4,0},{1,5},{5,1},{2,6},{6,2},{3,7},{7,3},{8,12},{12,8},{9,1... | collective-permute-start | bytes 3538952 | tf_op jit(solution)/shard_map/ppermute | solution.py:416
  57.3 4.8 %copy-start.12 = (bf16[2048,128]{1,0:T(8,128)(2,1)S(1)}, bf16[2048,128]{1,0:T(8,128)(2,1)}, u32[]{:S(2)}) copy-start(bf16[2048,128]{1,0:T(8,128)(2,1)} %param.4) | copy-start | bytes 1572868
  57.3 26.0 %all-to-all-start.2 = ((f32[64,4,1152]{2,1,0:T(4,128)}), f32[64,4,1152]{2,1,0:T(4,128)S(1)}, u32[]{:S(2)}, u32[]{:S(2)}) async-start(f32[64,4,1152]{2,1,0:T(4,128)} %broadcast_in_dim.10), calls=%async_computation.2 | async-start | bytes 2359296 | tf_op jit(solution)/shard_map/all_to_all | solution.py:396
  62.1 21.6 %copy-start.14 = (bf16[1024,128]{1,0:T(8,128)(2,1)}, bf16[1024,128]{1,0:T(8,128)(2,1)S(1)}, u32[]{:S(2)}) copy-start(bf16[1024,128]{1,0:T(8,128)(2,1)S(1)} %get-tuple-element.26.refs_4_) | copy-start | bytes 786436
  62.1 21.6 %copy-start.15 = (bf16[1024,128]{1,0:T(8,128)(2,1)}, bf16[1024,128]{1,0:T(8,128)(2,1)S(1)}, u32[]{:S(2)}) copy-start(bf16[1024,128]{1,0:T(8,128)(2,1)S(1)} %get-tuple-element.27.refs_0_) | copy-start | bytes 786436
  62.2 18.0 %collective-permute-start.4 = (bf16[1024,128]{1,0:T(8,128)(2,1)S(1)}, bf16[1024,128]{1,0:T(8,128)(2,1)S(1)}, u32[]{:S(2)}, u32[]{:S(2)}) collective-permute-start(bf16[1024,128]{1,0:T(8,128)(2,1)S(1)} %get-tuple-element.26.refs_4_), channel_id=1, source_target_pairs={{0,3},{1,0},{2,1},{3,2},{4,7},{5,4},{6,5},{7,6},{8,11},{9,8},{10,9... | collective-permute-start | bytes 786440 | tf_op jit(solution)/shard_map/ppermute | solution.py:407
  64.3 18.3 %collective-permute-start = (bf16[1024,128]{1,0:T(8,128)(2,1)S(1)}, bf16[1024,128]{1,0:T(8,128)(2,1)S(1)}, u32[]{:S(2)}, u32[]{:S(2)}) collective-permute-start(bf16[1024,128]{1,0:T(8,128)(2,1)S(1)} %get-tuple-element.27.refs_0_), channel_id=1, source_target_pairs={{0,1},{1,2},{2,3},{3,0},{4,5},{5,6},{6,7},{7,4},{8,9},{9,10},{10,1... | collective-permute-start | bytes 786440 | tf_op jit(solution)/shard_map/ppermute | solution.py:406
  64.3 23.9 %collective-permute-start.3 = (bf16[1024,128]{1,0:T(8,128)(2,1)S(1)}, bf16[1024,128]{1,0:T(8,128)(2,1)}, u32[]{:S(2)}, u32[]{:S(2)}) collective-permute-start(bf16[1024,128]{1,0:T(8,128)(2,1)S(1)} %get-tuple-element.26.refs_4_), channel_id=1, source_target_pairs={{0,1},{1,2},{2,3},{3,0},{4,5},{5,6},{6,7},{7,4},{8,9},{9,10},{10,1... | collective-permute-start | bytes 786440 | tf_op jit(solution)/shard_map/ppermute | solution.py:408
  64.6 23.6 %collective-permute-start.1 = (bf16[1024,128]{1,0:T(8,128)(2,1)S(1)}, bf16[1024,128]{1,0:T(8,128)(2,1)}, u32[]{:S(2)}, u32[]{:S(2)}) collective-permute-start(bf16[1024,128]{1,0:T(8,128)(2,1)S(1)} %get-tuple-element.27.refs_0_), channel_id=1, source_target_pairs={{0,3},{1,0},{2,1},{3,2},{4,7},{5,4},{6,5},{7,6},{8,11},{9,8},{10,9... | collective-permute-start | bytes 786440 | tf_op jit(solution)/shard_map/ppermute | solution.py:409
  80.2 3.6 %copy-start.16 = (bf16[1024,128]{1,0:T(8,128)(2,1)}, bf16[1024,128]{1,0:T(8,128)(2,1)S(1)}, u32[]{:S(2)}) copy-start(bf16[1024,128]{1,0:T(8,128)(2,1)S(1)} %collective-permute-done.4.refs_6_) | copy-start | bytes 786436
  80.2 11.3 %collective-permute-start.5 = (bf16[1024,128]{1,0:T(8,128)(2,1)S(1)}, bf16[1024,128]{1,0:T(8,128)(2,1)}, u32[]{:S(2)}, u32[]{:S(2)}) collective-permute-start(bf16[1024,128]{1,0:T(8,128)(2,1)S(1)} %collective-permute-done.4.refs_6_), channel_id=1, source_target_pairs={{0,3},{1,0},{2,1},{3,2},{4,7},{5,4},{6,5},{7,6},{8,11},{9,8},{10,9... | collective-permute-start | bytes 786440 | tf_op jit(solution)/shard_map/ppermute | solution.py:411
  82.7 1.1 copy-start.17
  82.7 11.0 %collective-permute-start.2 = (bf16[1024,128]{1,0:T(8,128)(2,1)S(1)}, bf16[1024,128]{1,0:T(8,128)(2,1)}, u32[]{:S(2)}, u32[]{:S(2)}) collective-permute-start(bf16[1024,128]{1,0:T(8,128)(2,1)S(1)} %collective-permute-done.refs_1_), channel_id=1, source_target_pairs={{0,1},{1,2},{2,3},{3,0},{4,5},{5,6},{6,7},{7,4},{8,9},{9,10},{10,1... | collective-permute-start | bytes 786440 | tf_op jit(solution)/shard_map/ppermute | solution.py:410
  83.8 24.9 %copy-start.13 = (f32[2,128,1152]{2,1,0:T(8,128)}, f32[2,128,1152]{2,1,0:T(8,128)S(1)}, u32[]{:S(2)}) copy-start(f32[2,128,1152]{2,1,0:T(8,128)S(1)} %reshape.27.refs_1_) | copy-start | bytes 3538948
  83.8 55.5 %collective-permute-start.7 = (f32[2,128,1152]{2,1,0:T(8,128)S(1)}, f32[2,128,1152]{2,1,0:T(8,128)}, u32[]{:S(2)}, u32[]{:S(2)}) collective-permute-start(f32[2,128,1152]{2,1,0:T(8,128)S(1)} %reshape.27.refs_1_), channel_id=1, source_target_pairs={{0,4},{4,0},{1,5},{5,1},{2,6},{6,2},{3,7},{7,3},{8,12},{12,8},{9,1... | collective-permute-start | bytes 3538952 | tf_op jit(solution)/shard_map/ppermute | solution.py:424
  130.4 4.1 %collective-permute-start.8 = (f32[64,256]{1,0:T(8,128)S(1)}, f32[64,256]{1,0:T(8,128)S(1)}, u32[]{:S(2)}, u32[]{:S(2)}) collective-permute-start(f32[64,256]{1,0:T(8,128)S(1)} %reduce_sum.19), channel_id=1, source_target_pairs={{0,4},{4,0},{1,5},{5,1},{2,6},{6,2},{3,7},{7,3},{8,12},{12,8},{9,1... | collective-permute-start | bytes 196616 | tf_op jit(solution)/shard_map/ppermute | solution.py:432
  135.6 43.3 %all-to-all-start.4 = ((f32[16,64,256]{2,1,0:T(8,128)}), f32[16,64,256]{2,1,0:T(8,128)S(1)}, u32[]{:S(2)}, u32[]{:S(2)}) async-start(f32[16,64,256]{2,1,0:T(8,128)} %broadcast_in_dim.22), calls=%async_computation.4 | async-start | bytes 2097152 | tf_op jit(solution)/shard_map/all_to_all | solution.py:396
  160.6 18.4 %copy-start.6 = (bf16[4,128,1024]{2,1,0:T(8,128)(2,1)S(1)}, bf16[4,128,1024]{2,1,0:T(8,128)(2,1)}, u32[]{:S(2)}) copy-start(bf16[4,128,1024]{2,1,0:T(8,128)(2,1)} %get-tuple-element.18.high0) | copy-start | bytes 3145732
  160.6 18.4 %copy-start.7 = (bf16[4,128,1024]{2,1,0:T(8,128)(2,1)S(1)}, bf16[4,128,1024]{2,1,0:T(8,128)(2,1)}, u32[]{:S(2)}) copy-start(bf16[4,128,1024]{2,1,0:T(8,128)(2,1)} %get-tuple-element.19.low0) | copy-start | bytes 3145732
  160.6 18.4 %copy-start.10 = (f32[4,128,128]{2,1,0:T(8,128)S(1)}, f32[4,128,128]{2,1,0:T(8,128)}, u32[]{:S(2)}) copy-start(f32[4,128,128]{2,1,0:T(8,128)} %get-tuple-element.20.inverse0) | copy-start | bytes 786436
  179.0 1.0 copy-start.8
  180.1 1.0 copy-start.9
  181.1 0.9 copy-start.11
  182.0 5.5 %copy-start = (f32[2048,256]{1,0:T(8,128)S(1)}, f32[2048,256]{1,0:T(8,128)}, u32[]{:S(2)}) copy-start(f32[2048,256]{1,0:T(8,128)} %residual.1) | copy-start | bytes 6291460
  182.1 5.5 %copy-start.4 = (bf16[2048,1024]{1,0:T(8,128)(2,1)S(1)}, bf16[2048,1024]{1,0:T(8,128)(2,1)}, u32[]{:S(2)}) copy-start(bf16[2048,1024]{1,0:T(8,128)(2,1)} %get-tuple-element.14.high) | copy-start | bytes 12582916
  182.1 5.5 %copy-start.5 = (bf16[2048,1024]{1,0:T(8,128)(2,1)S(1)}, bf16[2048,1024]{1,0:T(8,128)(2,1)}, u32[]{:S(2)}) copy-start(bf16[2048,1024]{1,0:T(8,128)(2,1)} %get-tuple-element.15.low) | copy-start | bytes 12582916
  187.6 1.2 copy-start.3
